TPU v7x, 32 devices: a whole 2x2x4 slice. The times are simulated.
32 devices in a mesh: dp: 16 (over z, y, core), mp: 2 (over x).
Axes of the slice: x: 2, y: 2, z: 4, core: 2. Of those that a mesh axis runs over, the one named last changes fastest.
Arguments:
- hidden: bfloat16 [512, 7168], P('dp', 'mp'), may hold values from -12 to 12
- steering: float32 [7168], P('mp'), may hold values from -3 to 3
- norm_gain: bfloat16 [7168], P('mp'), may hold values from 0.099609375 to 1.8984375
- target: bfloat16 [512, 7168], P('dp', 'mp'), may hold values from -8 to 8
- routes: int32 [512, 8], P('dp'), may hold values from 0 to 15, all different within a row; in each aligned block of 32 rows (0 to 31, 32 to 63, ...) at most 20 rows name the same one
- gate_probs: float32 [512, 8], P('dp'), may hold values from 0.05 to 0.3
- contrast: int32 [512], P('dp'), may hold values from 0 to 1
- gate_weight: bfloat16 [16, 7168, 2048], P('dp', None, 'mp'), may hold values from -0.0625 to 0.0625
- up_weight: bfloat16 [16, 7168, 2048], P('dp', None, 'mp'), may hold values from -0.0625 to 0.0625
- down_weight: bfloat16 [16, 2048, 7168], P('dp', 'mp'), may hold values from -0.125 to 0.125
Outputs:
- mixed: bfloat16 [512, 7168], P('dp', 'mp')
- steer_grad: float32 [7168], P('mp')
Inputs may be any that keep to these rules, and one draw needn't show every extreme that they name: `routes`: each row names 8 different experts; among the 32 rows of one index of dp no expert is named by more than 20 rows.
All inputs are finite; a program needn't handle non-finite values.
Results may differ from a plain program's by a relative error of at most 0.005.
Values may be sent and summed in bfloat16 or wider, within the bound.
No kernel may reach another device: no remote copies, remote signals or barrier semaphores. Data moves between devices by JAX's collectives and lax.ppermute only.
A program may use at most 128 MiB of HBM per device.

v0:
```python
import jax
import jax.numpy as jnp
from jax import lax
from jax.experimental import pallas as pl
from jax.experimental.pallas import tpu as pltpu
from jax.sharding import PartitionSpec as P

EPSILON = 1e-06
BF16 = jnp.bfloat16
F32 = jnp.float32
BOTH = ("dp", "mp")


def thirds(values):
    high = lax.reduce_precision(values, 8, 7)
    rest = values - high
    middle = lax.reduce_precision(rest, 8, 7)
    low = rest - middle
    return high.astype(BF16), middle.astype(BF16), low.astype(BF16)


def rows_times(values, matrix, contracted):
    rows = lax.optimization_barrier(jnp.stack(thirds(values)))
    return jnp.sum(
        lax.dot_general(rows, matrix, (((1,), (contracted,)), ((), ())), preferred_element_type=F32),
        axis=0,
    )


def forward(normed, gate_mat, up_mat):
    gate_pre = jnp.dot(normed, gate_mat, preferred_element_type=F32)
    up_pre = jnp.dot(normed, up_mat, preferred_element_type=F32)
    return lax.optimization_barrier((gate_pre, up_pre))


def outputs(gate_pre, up_pre, weight, down_mat):
    activated = lax.optimization_barrier((gate_pre * jax.nn.sigmoid(gate_pre) * up_pre).astype(BF16))
    out = jnp.dot(activated, down_mat, preferred_element_type=F32)
    return (out * weight).astype(BF16)


def pullback(gate_pre, up_pre, scale, inverse, rows, down_mat):
    back = lax.dot_general(rows, down_mat, (((1,), (1,)), ((), ())), preferred_element_type=F32)
    back = lax.optimization_barrier(back) * scale
    sigma = jax.nn.sigmoid(gate_pre)
    grad_gate = back * up_pre * sigma * (1.0 + gate_pre * (1.0 - sigma))
    grad_up = back * gate_pre * sigma
    share = jnp.sum(grad_gate * gate_pre + grad_up * up_pre, axis=1)
    return jnp.sum(grad_gate * inverse, axis=0), jnp.sum(grad_up * inverse, axis=0), share


def token_weights(routes, gate_probs, experts):
    named = routes[:, :, None] == jnp.arange(experts, dtype=jnp.int32)
    return jnp.sum(jnp.where(named, gate_probs[:, :, None], 0.0), axis=1)


def after(value, *others):
    return lax.optimization_barrier((value, *others))[0]


def tile_of(size, most):
    return max(t for t in range(128, most + 1, 128) if size % t == 0)


VMEM = pl.BlockSpec(memory_space=pltpu.VMEM)
SMEM = pl.BlockSpec(memory_space=pltpu.SMEM)
ANY = pl.BlockSpec(memory_space=pltpu.HBM)


def call(kernel, operands, specs, outs, scratch, megabytes, flops, moved):
    return pl.pallas_call(
        kernel,
        in_specs=specs,
        out_specs=[VMEM] * len(outs),
        out_shape=[jax.ShapeDtypeStruct(shape, dtype) for shape, dtype in outs],
        scratch_shapes=scratch,
        compiler_params=pltpu.CompilerParams(vmem_limit_bytes=megabytes << 20),
        cost_estimate=pl.CostEstimate(flops=flops, bytes_accessed=moved, transcendentals=0),
    )(*operands)


CHUNK = 16
WEIGHT, SIGNED, SQUARES, INVERSE = 0, 1, 2, 3


def column(array, index):
    return array[:, index : index + 1]


def facts_of(columns):
    rows = columns[0].shape[0]
    lane = lax.broadcasted_iota(jnp.int32, (rows, 128), 1)
    found = jnp.zeros((rows, 128), F32)
    for index, values in enumerate(columns):
        found = jnp.where(lane == index, values, found)
    return found


def scale_rows(blocks, steer, gain, scaled, squares):
    first, half = 0, scaled.shape[1]
    for source in blocks:
        group = next(g for g in (4, 2, 1) if source.shape[0] % (g * CHUNK) == 0)

        def chunks(number, carry, source=source, first=first, group=group):
            for k in range(group):
                at = pl.multiple_of((number * group + k) * CHUNK, CHUNK)
                stream = source[pl.ds(at, CHUNK), :half].astype(F32) + steer
                scaled[pl.ds(first + at, CHUNK), :] = (stream * gain).astype(BF16)
                square = stream * stream
                squares[pl.ds(first + at, CHUNK), :] = sum(square[:, c : c + 128] for c in range(0, half, 128))
            return carry

        lax.fori_loop(0, source.shape[0] // (group * CHUNK), chunks, 0)
        first += source.shape[0]


def fetches(source, buffer, sems, view, ahead=2):
    count = buffer.shape[0]
    copies = lambda i: pltpu.make_async_copy(view(source, i), buffer.at[i], sems.at[i])
    for i in range(min(ahead, count)):
        copies(i).start()

    def take(i):
        copies(i).wait()

        @pl.when(i + ahead < count)
        def _():
            copies(i + ahead).start()

    return take


def split_dot(rows, matrix):
    middle = rows.shape[0] // 2
    return jnp.concatenate(
        [jnp.dot(rows[part, :], matrix, preferred_element_type=F32) for part in (slice(0, middle), slice(middle, None))], axis=0
    )


def half_fetches(gate_mat, up_mat, gate_buf, up_buf, gate_sems, up_sems, chosen):
    tile = gate_buf.shape[2]
    view = lambda source, i: source.at[chosen, :, pl.ds(i * tile, tile)]
    return fetches(gate_mat, gate_buf, gate_sems, view), fetches(up_mat, up_buf, up_sems, view)


def own_kernel(experts, which, a, b, c, d, steer, gain, gate_mat, up_mat, gate_acc, up_acc, scaled, facts, gate_buf, up_buf, gate_sems, up_sems, squares):
    gate_wait, up_wait = half_fetches(gate_mat, up_mat, gate_buf, up_buf, gate_sems, up_sems, which[0])
    half, tile = scaled.shape[1], gate_buf.shape[2]
    scale_rows((a, b, c, d), steer[which[0]], gain[which[0]], scaled, squares)
    first = 0
    for source in (a, b, c, d):
        rows = slice(first, first + source.shape[0])
        values = source[:, half:].astype(F32)
        lane = lax.broadcasted_iota(jnp.int32, values.shape, 1)
        mine = (lane == which[2]) | (lane == which[2] + experts) | (lane == which[2] + 2 * experts)
        weight = jnp.sum(jnp.where(mine, values, 0.0), axis=1, keepdims=True)
        sign = jnp.sum(jnp.where(lane == 3 * experts, values, 0.0), axis=1, keepdims=True)
        facts[rows, :] = facts_of([weight, weight * sign, jnp.sum(squares[rows, :], axis=1, keepdims=True)])
        first += source.shape[0]

    def step(i, carry):
        at = pl.ds(pl.multiple_of(i * tile, tile), tile)
        gate_wait(i)
        gate_acc[:, at] = split_dot(scaled, gate_buf[i])
        up_wait(i)
        up_acc[:, at] = split_dot(scaled, up_buf[i])
        return carry

    lax.fori_loop(0, gate_buf.shape[0], step, 0)


def other_kernel(which, a, b, c, d, steer, gain, gate_mat, up_mat, gate_acc, up_acc, facts, gate_pre, up_pre, activated, scaled, found, gate_buf, up_buf, gate_sems, up_sems, squares):
    gate_wait, up_wait = half_fetches(gate_mat, up_mat, gate_buf, up_buf, gate_sems, up_sems, which[1])
    half, tile = scaled.shape[1], gate_buf.shape[2]
    scale_rows((a, b, c, d), steer[which[1]], gain[which[1]], scaled, squares)
    old = facts[...]
    total = column(old, SQUARES) + jnp.sum(squares[...], axis=1, keepdims=True)
    found[...] = facts_of([column(old, WEIGHT), column(old, SIGNED), total, lax.rsqrt(total / (2 * half) + EPSILON)])

    def step(i, carry):
        at = pl.ds(pl.multiple_of(i * tile, tile), tile)
        inverse = column(found[...], INVERSE)
        gate_wait(i)
        gate = (gate_acc[:, at] + split_dot(scaled, gate_buf[i])) * inverse
        gate_pre[:, at] = gate
        up_wait(i)
        up = (up_acc[:, at] + split_dot(scaled, up_buf[i])) * inverse
        up_pre[:, at] = up
        activated[:, at] = (gate * jax.nn.sigmoid(gate) * up).astype(BF16)
        return carry

    lax.fori_loop(0, gate_buf.shape[0], step, 0)


def half_products(which, blocks, steer, gain, gate_mat, up_mat, state=None):
    half, units = gate_mat.shape[1:]
    rows, tile = sum(b.shape[0] for b in blocks), tile_of(units, 256)
    unit, wide = ((rows, units), F32), ((rows, half), BF16)
    facts = (rows, 128), F32
    buffer, sems = pltpu.VMEM((units // tile, half, tile), BF16), pltpu.SemaphoreType.DMA((units // tile,))
    operands = [which, *blocks, steer, gain, gate_mat, up_mat]
    specs = [SMEM] + [VMEM] * 6 + [ANY] * 2
    if state is None:
        experts = lax.axis_size("dp")
        kernel = lambda *refs: own_kernel(experts, *refs)
        outs = [unit, unit, wide, facts]
    else:
        kernel = other_kernel
        operands += state
        specs += [VMEM] * 3
        outs = [unit, unit, ((rows, units), BF16), wide, facts]
    return call(
        kernel,
        operands,
        specs,
        outs,
        [buffer, buffer, sems, sems, pltpu.VMEM((rows, 128), F32)],
        44,
        4 * rows * half * units,
        4 * half * units,
    )


def out_kernel(chosen, which, activated, facts, down_mat, near, far, buf, sems):
    tile, height = buf.shape[2], near.shape[0]
    tiles = buf.shape[0]
    start = which[chosen] * (tile * tiles)
    wait = fetches(down_mat, buf, sems, lambda source, i: source.at[:, pl.ds(pl.multiple_of(start + i * tile, tile), tile)], 3)

    def step(i, carry):
        at = pl.ds(pl.multiple_of(i * tile, tile), tile)
        wait(i)
        out = split_dot(activated, buf[i]) * column(facts[...], WEIGHT)
        near[:, at] = out[:height].astype(BF16)
        far[:, at] = out[height:].astype(BF16)
        return carry

    lax.fori_loop(0, tiles, step, 0)


def expert_out(chosen, which, activated, facts, down_mat):
    rows, units = activated.shape
    half = down_mat.shape[1] // 2
    tile = tile_of(half, 512)
    out = ((rows // 2, half), BF16)
    return call(
        lambda *refs: out_kernel(chosen, *refs),
        (which, activated, facts, down_mat),
        [SMEM, VMEM, VMEM, ANY],
        [out, out],
        [pltpu.VMEM((half // tile, units, tile), BF16), pltpu.SemaphoreType.DMA((half // tile,))],
        44,
        2 * rows * half * units,
        2 * half * units,
    )


def back_kernel(which, near_own, far_own, near_other, far_other, gate_pre, up_pre, facts, down_mat, gate_sum, up_sum, share, own_buf, other_buf, own_sems, other_sems):
    tile, half = own_buf.shape[1:]
    view = lambda h: lambda source, i: source.at[pl.ds(i * tile, tile), pl.ds(pl.multiple_of(which[h] * half, half), half)]
    own_take = fetches(down_mat, own_buf, own_sems, view(0))
    other_take = fetches(down_mat, other_buf, other_sems, view(1))
    dims = (((1,), (1,)), ((), ()))
    share[...] = jnp.zeros_like(share)
    height = near_own.shape[0]

    def step(i, carry):
        at = pl.ds(pl.multiple_of(i * tile, tile), tile)
        own_take(i)
        other_take(i)
        gate_total, up_total = 0.0, 0.0
        for first, own, other in ((0, near_own, near_other), (height, far_own, far_other)):
            rows = slice(first, first + height)
            known = facts[rows, :]
            back = lax.dot_general(own[...], own_buf[i], dims, preferred_element_type=F32)
            back += lax.dot_general(other[...], other_buf[i], dims, preferred_element_type=F32)
            back *= column(known, SIGNED)
            gate, up = gate_pre[rows, at], up_pre[rows, at]
            sigma = jax.nn.sigmoid(gate)
            grad_gate = back * up * sigma * (1.0 + gate * (1.0 - sigma))
            grad_up = back * gate * sigma
            inverse = column(known, INVERSE)
            gate_total += jnp.sum(grad_gate * inverse, axis=0, keepdims=True)
            up_total += jnp.sum(grad_up * inverse, axis=0, keepdims=True)
            part = grad_gate * gate + grad_up * up
            share[rows, :] += sum(part[:, c : c + 128] for c in range(0, tile, 128))
        gate_sum[:, at] = gate_total
        up_sum[:, at] = up_total
        return carry

    lax.fori_loop(0, own_buf.shape[0], step, 0)


def expert_back(which, rows_of, down_mat, gate_pre, up_pre, facts):
    half = rows_of[0].shape[1]
    rows, units = gate_pre.shape
    tile = tile_of(units, 256)
    buffer, sems = pltpu.VMEM((units // tile, tile, half), BF16), pltpu.SemaphoreType.DMA((units // tile,))
    return call(
        back_kernel,
        (which, *rows_of, gate_pre, up_pre, facts, down_mat),
        [SMEM] + [VMEM] * 7 + [ANY],
        [((1, units), F32), ((1, units), F32), ((rows, 128), F32)],
        [buffer, buffer, sems, sems],
        44,
        4 * rows * half * units,
        4 * half * units,
    )


def through_kernel(gate_sum, up_sum, gate_mat, up_mat, out, gate_buf, up_buf, gate_sems, up_sems):
    tiles, tile, units = gate_buf.shape
    view = lambda source, i: source.at[pl.ds(i * tile, tile), :]
    gate_wait = fetches(gate_mat, gate_buf, gate_sems, view)
    up_wait = fetches(up_mat, up_buf, up_sems, view)
    chunk = 128

    def step(i, carry):
        gate_wait(i)
        up_wait(i)

        for r in range(tile // chunk):
            at = pl.ds(r * chunk, chunk)
            total = jnp.zeros((chunk, 128), F32)
            for c in range(0, units, 128):
                lanes = slice(c, c + 128)
                total += gate_buf[i, at, lanes].astype(F32) * gate_sum[:, lanes]
                total += up_buf[i, at, lanes].astype(F32) * up_sum[:, lanes]
            to = pl.ds(pl.multiple_of(i * tile + r * chunk, chunk), chunk)
            out[:, to] = jnp.sum(total.T, axis=0, keepdims=True)
        return carry

    lax.fori_loop(0, tiles, step, 0)


def through_weights(gate_sum, up_sum, gate_mat, up_mat):
    full, units = gate_mat.shape
    tile = tile_of(full, 896)
    buffer, sems = pltpu.VMEM((full // tile, tile, units), BF16), pltpu.SemaphoreType.DMA((full // tile,))
    return call(
        through_kernel,
        (gate_sum, up_sum, gate_mat, up_mat),
        [VMEM, VMEM, ANY, ANY],
        [((1, full), F32)],
        [buffer, buffer, sems, sems],
        48,
        512 * full * units,
        4 * full * units,
    )[0]


def fast_body(hidden, steering, norm_gain, target, routes, gate_probs, contrast, gate_weight, up_weight, down_weight):
    tokens, half = hidden.shape
    devices = 2 * lax.axis_size("dp")
    experts = lax.axis_size("dp")
    full = 2 * half
    gate_mat, up_mat, down_mat = gate_weight[0], up_weight[0], down_weight[0]
    gate_halves = gate_mat.reshape(2, half, gate_mat.shape[1])
    up_halves = up_mat.reshape(2, half, up_mat.shape[1])
    here, side = lax.axis_index("dp"), lax.axis_index("mp")
    even = here % 2 == 0
    low_side = side == 0
    which = jnp.stack([side, 1 - side, here]).astype(jnp.int32)
    top = devices.bit_length() - 1
    falling = [1 << b for b in range(top - 1, 2, -1)]
    orders = (falling + [1 << 2, 1], [1 << 2] + falling[:-1] + [1, falling[-1]])
    steps = len(falling) + 2
    last, third = steps - 1, steps - 2

    def permute(value, mask):
        return lax.ppermute(value, BOTH, [(i, i ^ mask(i)) for i in range(devices)])

    def hop(value, step):
        return permute(value, lambda i: orders[(i >> 1) & 1][step])

    def swap(value):
        return permute(value, lambda i: 2)

    def cross(value):
        return permute(value, lambda i: 1)

    def spread(value, gates=None):
        hold = (lambda v, g: after(v, *gates[g])) if gates else (lambda v, g: v)
        held = hold(value, 0)
        for step in range(steps - 3):
            held = jnp.concatenate([held, hop(held, step)], axis=0)
        p0 = hold(held, 1)
        p1 = hop(p0, steps - 3)
        p4 = hop(p0, last)
        p2 = hop(p0, third)
        p1, p2 = hold(p1, 2), hold(p2, 2)
        p3 = hop(p1, third)
        p5 = hop(p1, last)
        p6 = hop(p2, last)
        p7 = hop(hold(p3, 3), last)
        join = lambda a, b: jnp.concatenate([a, b], axis=0)
        own_a = join(p0, p1)
        own_b = join(jnp.where(even, p2, p4), jnp.where(even, p3, p5))
        other_a = join(jnp.where(even, p4, p2), jnp.where(even, p5, p3))
        return [own_a, own_b, other_a, join(p6, p7)], ((p3, p5), (p6, p7))

    gain = norm_gain.astype(F32)
    sign = (2 * contrast - 1).astype(F32)
    weights = token_weights(routes, gate_probs, experts)
    meta = jnp.concatenate([*thirds(weights), sign.astype(BF16)[:, None]], axis=1)
    meta = jnp.pad(meta, ((0, 0), (0, 128 - meta.shape[1])))
    vectors = jnp.stack([steering, gain])
    vectors_other = cross(vectors)
    steer_halves = jnp.where(low_side, jnp.stack([vectors[0], vectors_other[0]]), jnp.stack([vectors_other[0], vectors[0]]))
    gain_halves = jnp.where(low_side, jnp.stack([vectors[1], vectors_other[1]]), jnp.stack([vectors_other[1], vectors[1]]))
    steer_halves, gain_halves = steer_halves[:, None, :], gain_halves[:, None, :]

    (own_a, own_b, other_a, other_b), arrived = spread(jnp.concatenate([hidden, meta], axis=1))
    shared = (steer_halves, gain_halves, gate_halves, up_halves)
    gate_acc, up_acc, own_scaled, facts = half_products(which, (own_a, own_b, swap(own_a), swap(own_b)), *shared)
    other_far_a = swap(other_a)
    other_b = after(other_b, facts)
    gate_pre, up_pre, activated, other_scaled, facts = half_products(
        which, (other_a, other_b, other_far_a, swap(other_b)), *shared, (gate_acc, up_acc, facts)
    )
    near_other, far_other = expert_out(1, which, activated, facts, down_mat)
    here_other = swap(far_other)
    near_own, far_own = expert_out(0, which, after(activated, near_other), facts, down_mat)
    here_own = swap(far_own)

    targets, _ = spread(target, (*arrived, (activated,), (near_other,)))

    def add(*addends):
        return sum(a.astype(F32) for a in addends).astype(BF16)

    rows = near_own.shape[0] // 4
    sum_own, sum_other = (near_own, here_own), (near_other, here_other)
    piece = lambda pair, i: add(*(v[i * rows : (i + 1) * rows] for v in pair))
    a7, a6 = piece(sum_other, 3), piece(sum_other, 2)
    a5 = jnp.where(even, piece(sum_other, 1), piece(sum_own, 3))
    a4 = jnp.where(even, piece(sum_other, 0), piece(sum_own, 2))
    a3 = jnp.where(even, piece(sum_own, 3), piece(sum_other, 1))
    a2 = jnp.where(even, piece(sum_own, 2), piece(sum_other, 0))
    a1, a0 = piece(sum_own, 1), piece(sum_own, 0)
    b3 = hop(a7, last)
    b2 = hop(a6, last)
    b1 = hop(a5, last)
    b0 = hop(a4, last)
    third1, third0 = add(a3, b3), add(a2, b2)
    c1 = hop(third1, third)
    c0 = hop(third0, third)
    early = add(a1, b1, c1)
    d0 = hop(early, steps - 3)
    addends = [a0, b0, c0, d0]
    for step in range(steps - 4, -1, -1):
        rows //= 2
        addends.append(hop(add(*(a[rows : 2 * rows] for a in addends)), step))
    out_tok = sum(a[:tokens].astype(F32) for a in addends)
    mixed = (hidden.astype(F32) + steering[None, :] + out_tok).astype(BF16)

    own_a, own_b, other_a, other_b = targets
    target_own = jnp.concatenate([own_a, own_b], axis=0)
    target_other = jnp.concatenate([other_a, other_b], axis=0)
    far = swap(target_own), swap(target_other)
    rows_of = after(target_own, a7, a6, a5, a4), far[0], target_other, far[1]
    gate_sum, up_sum, share = expert_back(which, rows_of, down_mat, gate_pre, up_pre, facts)
    through = through_weights(after(gate_sum, third1, third0), up_sum, gate_mat, up_mat)[0]
    along = jnp.sum(after(share, early), axis=1) * facts[:, INVERSE] * facts[:, INVERSE]
    along_own, along_other = rows_times(along, own_scaled, 0), rows_times(along, other_scaled, 0)
    low_part, high_part = through[:half], through[half:]
    through_own = jnp.where(low_side, low_part, high_part)
    through_other = jnp.where(low_side, high_part, low_part)
    finish = lambda through, along, gain: gain * through - along / (gain * full)
    grad = finish(through_own, along_own, gain) + cross(finish(through_other, along_other, vectors_other[1]))
    grad = grad + jnp.sum(target.astype(F32) * sign[:, None], axis=0)
    bits = [1 << bit for bit in range(1, top)]
    for group in (bits[:2], bits[2:4], *([bit] for bit in bits[4:])):
        masks = [sum(bit for k, bit in enumerate(group) if n >> k & 1) for n in range(1, 1 << len(group))]
        grad = sum([permute(grad, lambda i, mask=mask: mask) for mask in masks], grad)
    return mixed, grad


def general_body(hidden, steering, norm_gain, target, routes, gate_probs, contrast, gate_weight, up_weight, down_weight):
    _, width = hidden.shape
    groups, parts = lax.axis_size("dp"), lax.axis_size("mp")
    local_experts = gate_weight.shape[0]
    full = width * parts
    here, side = lax.axis_index("dp"), lax.axis_index("mp")

    def gather(value):
        return lax.all_gather(lax.all_gather(value, "mp", axis=1, tiled=True), "dp", axis=0, tiled=True)

    sign = (2 * contrast - 1).astype(F32)
    weights = token_weights(routes, gate_probs, local_experts * groups)
    facts = lax.all_gather(jnp.concatenate([weights, sign[:, None]], axis=1), "dp", axis=0, tiled=True)
    steer_row = lax.all_gather(steering, "mp", axis=0, tiled=True)[None, :]
    gain_row = lax.all_gather(norm_gain.astype(F32), "mp", axis=0, tiled=True)[None, :]
    stream = gather(hidden).astype(F32) + steer_row
    inverse = lax.rsqrt(jnp.mean(stream * stream, axis=1, keepdims=True) + EPSILON)
    normed = (stream * inverse * gain_row).astype(BF16)
    all_target = gather(target)
    out, through, share = 0.0, 0.0, 0.0
    for k in range(local_experts):
        weight = lax.dynamic_index_in_dim(facts, here * local_experts + k, axis=1)
        gate_pre, up_pre = forward(normed, gate_weight[k], up_weight[k])
        out = out + outputs(gate_pre, up_pre, weight, down_weight[k]).astype(F32)
        vg, vu, part = pullback(gate_pre, up_pre, weight * facts[:, -1:], inverse, all_target, down_weight[k])
        through = through + rows_times(vg, gate_weight[k], 1) + rows_times(vu, up_weight[k], 1)
        share = share + part
    out = lax.psum_scatter(out.astype(BF16), "mp", scatter_dimension=1, tiled=True)
    out_tok = lax.psum_scatter(out, "dp", scatter_dimension=0, tiled=True).astype(F32)
    mixed = (hidden.astype(F32) + steering[None, :] + out_tok).astype(BF16)
    along = rows_times(share * inverse[:, 0], normed, 0)
    partial = gain_row[0] * through - along / (gain_row[0] * full)
    own = jnp.sum(target.astype(F32) * sign[:, None], axis=0)
    grad = lax.psum(partial, "mp")
    grad = lax.dynamic_slice_in_dim(grad, side * width, width) + own
    return mixed, lax.psum(grad, "dp")


def solution(mesh):
    groups, parts = mesh.shape["dp"], mesh.shape["mp"]
    fast = parts == 2 and 8 <= groups <= 32 and groups & (groups - 1) == 0

    def body(*args):
        if fast and args[7].shape[0] == 1:
            return fast_body(*args)
        return general_body(*args)

    placed = (
        P("dp", "mp"),
        P("mp"),
        P("mp"),
        P("dp", "mp"),
        P("dp", None),
        P("dp", None),
        P("dp"),
        P("dp", None, "mp"),
        P("dp", None, "mp"),
        P("dp", "mp", None),
    )
    return jax.shard_map(
        body, mesh=mesh, in_specs=placed, out_specs=(P("dp", "mp"), P("mp")), check_vma=False
    )
```

profile of v0, /device:TPU:0, one launch (start us, length us, event | category | flops | bytes accessed | tf_op | source)
XLA Modules:
  0.0 210.8 jit_solution(2438833220463249883)
XLA Ops:
  3.4 4.1 %collective-permute-start = (bf16[32,3712]{1,0:T(8,128)(2,1)S(1)}, bf16[32,3712]{1,0:T(8,128)(2,1)S(1)}, u32[]{:S(2)}, u32[]{:S(2)}) collective-permute-start(bf16[32,3712]{1,0:T(8,128)(2,1)S(1)} %pad_maximum_fusion.8), channel_id=1, source_target_pairs={{0,16},{1,17},{2,6},{3,7},{4,20},{5,21},{6,2},{7,3},{8,24},{9,25},... | collective-permute-start | bytes 712712 | tf_op jit(solution)/shard_map/ppermute | solution.py:371
  9.0 1.6 collective-permute-start.10
  12.1 2.1 collective-permute-done
  15.1 1.1 collective-permute-start.3
  16.2 1.5 collective-permute-start.2
  17.7 1.5 collective-permute-start.1
  19.2 12.1 %collective-permute-done.3 = bf16[64,3712]{1,0:T(8,128)(2,1)S(1)} collective-permute-done((bf16[64,3712]{1,0:T(8,128)(2,1)S(1)}, bf16[64,3712]{1,0:T(8,128)(2,1)S(1)}, u32[]{:S(2)}, u32[]{:S(2)}) %collective-permute-start.3) | collective-permute-done | bytes 475168 | tf_op jit(solution)/shard_map/ppermute | solution.py:371
  31.5 1.6 collective-permute-start.5
  33.6 1.5 collective-permute-start.6
  35.2 5.0 %collective-permute-done.5 = bf16[64,3712]{1,0:T(8,128)(2,1)S(1)} collective-permute-done((bf16[64,3712]{1,0:T(8,128)(2,1)S(1)}, bf16[64,3712]{1,0:T(8,128)(2,1)S(1)}, u32[]{:S(2)}, u32[]{:S(2)}) %collective-permute-start.5) | collective-permute-done | bytes 475168 | tf_op jit(solution)/shard_map/ppermute | solution.py:371
  40.2 4.6 %collective-permute-done.4 = bf16[64,3712]{1,0:T(8,128)(2,1)S(1)} collective-permute-done((bf16[64,3712]{1,0:T(8,128)(2,1)S(1)}, bf16[64,3712]{1,0:T(8,128)(2,1)S(1)}, u32[]{:S(2)}, u32[]{:S(2)}) %collective-permute-start.4) | collective-permute-done | bytes 475168 | tf_op jit(solution)/shard_map/ppermute | solution.py:371
  46.1 3.7 %collective-permute-done.6 = bf16[64,3712]{1,0:T(8,128)(2,1)S(1)} collective-permute-done((bf16[64,3712]{1,0:T(8,128)(2,1)S(1)}, bf16[64,3712]{1,0:T(8,128)(2,1)S(1)}, u32[]{:S(2)}, u32[]{:S(2)}) %collective-permute-start.6) | collective-permute-done | bytes 475168 | tf_op jit(solution)/shard_map/ppermute | solution.py:371
  49.8 5.1 %collective-permute-done.7 = bf16[64,3712]{1,0:T(8,128)(2,1)S(1)} collective-permute-done((bf16[64,3712]{1,0:T(8,128)(2,1)S(1)}, bf16[64,3712]{1,0:T(8,128)(2,1)S(1)}, u32[]{:S(2)}, u32[]{:S(2)}) %collective-permute-start.7) | collective-permute-done | bytes 475168 | tf_op jit(solution)/shard_map/ppermute | solution.py:371
  55.0 12.3 %shard_map.113 = (f32[512,1024]{1,0:T(8,128)S(1)}, f32[512,1024]{1,0:T(8,128)S(1)}, bf16[512,3584]{1,0:T(8,128)(2,1)}, f32[512,128]{1,0:T(8,128)S(1)}) custom-call(s32[3]{0:T(128)S(1)} %pad_add_fusion.refs_0_.which, bf16[128,3712]{1,0:T(8,128)(2,1)S(1)} %pad_maximum_fusion.4.refs_1_, bf16[128,3712]{1,0:T(8,128)(2,1)S(1)} %pad_maximum_fusion.5.refs_2_, ...), custom_call_target="tpu_custom_call" | custom-call | flops 7516192768 | bytes 14680064 | tf_op jit(solution)/shard_map/pallas_call | solution.py:71
  67.4 1.4 copy-done
  68.8 1.3 copy-done.1
  70.7 8.4 %collective-permute-done.23 = bf16[32,3584]{1,0:T(8,128)(2,1)S(1)} collective-permute-done((bf16[32,3584]{1,0:T(8,128)(2,1)S(1)}, bf16[32,3584]{1,0:T(8,128)(2,1)S(1)}, u32[]{:S(2)}, u32[]{:S(2)}) %collective-permute-start.23) | collective-permute-done | bytes 229408 | tf_op jit(solution)/shard_map/ppermute | solution.py:371
  79.1 1.0 collective-permute-start.26
  80.1 1.6 collective-permute-start.25
  81.7 14.4 %shard_map.114 = (f32[512,1024]{1,0:T(8,128)S(1)}, f32[512,1024]{1,0:T(8,128)S(1)}, bf16[512,1024]{1,0:T(8,128)(2,1)S(1)}, bf16[512,3584]{1,0:T(8,128)(2,1)}, f32[512,128]{1,0:T(8,128)S(1)}) custom-call(s32[3]{0:T(128)S(1)} %pad_add_fusion.refs_0_.which, bf16[128,3712]{1,0:T(8,128)(2,1)S(1)} %pad_maximum_fusion.2.a, ...), custom_call_target="tpu_custom_call" | custom-call | flops 7516192768 | bytes 14680064 | tf_op jit(solution)/shard_map/pallas_call | solution.py:71
  96.1 1.1 collective-permute-start.28
  97.8 8.1 %shard_map.115 = (bf16[256,3584]{1,0:T(8,128)(2,1)S(1)}, bf16[256,3584]{1,0:T(8,128)(2,1)}) custom-call(s32[3]{0:T(128)S(1)} %pad_add_fusion.refs_0_.which, bf16[512,1024]{1,0:T(8,128)(2,1)S(1)} %get-tuple-element.35.refs_1_, f32[512,128]{1,0:T(8,128)S(1)} %get-tuple-element.33.refs_2_.facts, bf16[1024,7168]{1,0:T(8,128)(2,1)} %bitcast.26), custom_call_target="tpu_custom_call" | custom-call | flops 3758096384 | bytes 7340032 | tf_op jit(solution)/shard_map/pallas_call | solution.py:71
  105.9 6.8 %shard_map.116 = (bf16[256,3584]{1,0:T(8,128)(2,1)S(1)}, bf16[256,3584]{1,0:T(8,128)(2,1)S(1)}) custom-call(s32[3]{0:T(128)S(1)} %pad_add_fusion.refs_0_.which, bf16[512,1024]{1,0:T(8,128)(2,1)S(1)} %get-tuple-element.35.refs_1_, f32[512,128]{1,0:T(8,128)S(1)} %get-tuple-element.33.refs_2_.facts, bf16[1024,7168]{1,0:T(8,128)(2,1)} %bitcast.27), custom_call_target="tpu_custom_call" | custom-call | flops 3758096384 | bytes 7340032 | tf_op jit(solution)/shard_map/pallas_call | solution.py:71
  114.3 1.2 collective-permute-start.31
  115.8 6.0 %collective-permute-done.30 = bf16[64,3584]{1,0:T(8,128)(2,1)S(1)} collective-permute-done((bf16[64,3584]{1,0:T(8,128)(2,1)S(1)}, bf16[64,3584]{1,0:T(8,128)(2,1)S(1)}, u32[]{:S(2)}, u32[]{:S(2)}) %collective-permute-start.30) | collective-permute-done | bytes 458784 | tf_op jit(solution)/shard_map/ppermute | solution.py:371
  121.8 4.9 %collective-permute-done.31 = bf16[64,3584]{1,0:T(8,128)(2,1)S(1)} collective-permute-done((bf16[64,3584]{1,0:T(8,128)(2,1)S(1)}, bf16[64,3584]{1,0:T(8,128)(2,1)S(1)}, u32[]{:S(2)}, u32[]{:S(2)}) %collective-permute-start.31) | collective-permute-done | bytes 458784 | tf_op jit(solution)/shard_map/ppermute | solution.py:371
  126.9 1.4 add_convert_fusion.7
  129.4 1.1 collective-permute-start.19
  130.5 1.7 broadcast_select_fusion.9
  133.2 3.8 %collective-permute-done.16 = bf16[64,3584]{1,0:T(8,128)(2,1)S(1)} collective-permute-done((bf16[64,3584]{1,0:T(8,128)(2,1)S(1)}, bf16[64,3584]{1,0:T(8,128)(2,1)S(1)}, u32[]{:S(2)}, u32[]{:S(2)}) %collective-permute-start.16) | collective-permute-done | bytes 458784 | tf_op jit(solution)/shard_map/ppermute | solution.py:371
  136.9 4.9 %collective-permute-done.19 = bf16[64,3584]{1,0:T(8,128)(2,1)S(1)} collective-permute-done((bf16[64,3584]{1,0:T(8,128)(2,1)S(1)}, bf16[64,3584]{1,0:T(8,128)(2,1)S(1)}, u32[]{:S(2)}, u32[]{:S(2)}) %collective-permute-start.19) | collective-permute-done | bytes 458784 | tf_op jit(solution)/shard_map/ppermute | solution.py:371
  141.8 1.9 add_convert_fusion.6
  143.8 1.6 collective-permute-start.20
  145.7 1.1 collective-permute-start.15
  147.2 1.5 collective-permute-start.17
  148.7 3.6 %collective-permute-done.20 = bf16[64,3584]{1,0:T(8,128)(2,1)S(1)} collective-permute-done((bf16[64,3584]{1,0:T(8,128)(2,1)S(1)}, bf16[64,3584]{1,0:T(8,128)(2,1)S(1)}, u32[]{:S(2)}, u32[]{:S(2)}) %collective-permute-start.20) | collective-permute-done | bytes 458784 | tf_op jit(solution)/shard_map/ppermute | solution.py:371
  152.3 1.0 add_convert_fusion
  153.3 1.9 collective-permute-start.21
  155.3 13.2 %shard_map.117 = (f32[1,1024]{1,0:T(1,128)S(1)}, f32[1,1024]{1,0:T(1,128)S(1)}, f32[512,128]{1,0:T(8,128)S(1)}) custom-call(s32[3]{0:T(128)S(1)} %pad_add_fusion.refs_0_.which, bf16[256,3584]{1,0:T(8,128)(2,1)S(1)} %pad_maximum_fusion.near_own, bf16[256,3584]{1,0:T(8,128)(2,1)S(1)} %collective-permute-done.29.far_own, ...), custom_call_target="tpu_custom_call" | custom-call | flops 7516192768 | bytes 14680064 | tf_op jit(solution)/shard_map/pallas_call | solution.py:71
  168.7 2.6 %convolution_reduce_fusion = f32[3584]{0:T(1024)S(1)} fusion(bf16[3,512]{1,0:T(4,128)(2,1)S(1)} %pad_maximum_fusion.10, bf16[512,3584]{1,0:T(8,128)(2,1)} %get-tuple-element.53), kind=kOutput, calls=%fused_computation.2 | convolution fusion | flops 11017216 | bytes 3687424 | tf_op jit(solution)/shard_map/dot_general | solution.py:25
  171.4 10.7 %shard_map.118 = f32[1,7168]{1,0:T(1,128)S(1)} custom-call(f32[1,1024]{1,0:T(1,128)S(1)} %get-tuple-element.48.gate_sum, f32[1,1024]{1,0:T(1,128)S(1)} %get-tuple-element.49.up_sum, bf16[7168,1024]{1,0:T(8,128)(2,1)} %bitcast.22, bf16[7168,1024]{1,0:T(8,128)(2,1)} %bitcast.25), custom_call_target="tpu_custom_call" | custom-call | flops 3758096384 | bytes 29360128 | tf_op jit(solution)/shard_map/pallas_call | solution.py:71
  183.9 2.2 %collective-permute-done.33 = f32[3584]{0:T(1024)S(1)} collective-permute-done((f32[3584]{0:T(1024)S(1)}, f32[3584]{0:T(1024)S(1)}, u32[]{:S(2)}, u32[]{:S(2)}) %collective-permute-start.33) | collective-permute-done | bytes 14368 | tf_op jit(solution)/shard_map/ppermute | solution.py:371
  186.1 6.6 %collective-permute-start.36 = (f32[3584]{0:T(1024)S(1)}, f32[3584]{0:T(1024)S(1)}, u32[]{:S(2)}, u32[]{:S(2)}) collective-permute-start(f32[3584]{0:T(1024)S(1)} %add_add_fusion.2), channel_id=1, source_target_pairs={{0,6},{1,7},{2,4},{3,5},{4,2},{5,3},{6,0},{7,1},{8,14},{9,15},{10,... | collective-permute-start | bytes 43016 | tf_op jit(solution)/shard_map/ppermute | solution.py:371
  192.7 1.5 collective-permute-done.36
  194.2 2.3 %collective-permute-done.35 = f32[3584]{0:T(1024)S(1)} collective-permute-done((f32[3584]{0:T(1024)S(1)}, f32[3584]{0:T(1024)S(1)}, u32[]{:S(2)}, u32[]{:S(2)}) %collective-permute-start.35) | collective-permute-done | bytes 14368 | tf_op jit(solution)/shard_map/ppermute | solution.py:371
  196.6 1.4 collective-permute-start.38
  198.1 2.8 %collective-permute-start.37 = (f32[3584]{0:T(1024)S(1)}, f32[3584]{0:T(1024)S(1)}, u32[]{:S(2)}, u32[]{:S(2)}) collective-permute-start(f32[3584]{0:T(1024)S(1)} %add_add_fusion.1), channel_id=1, source_target_pairs={{0,8},{1,9},{2,10},{3,11},{4,12},{5,13},{6,14},{7,15},{8,0},{9,1},... | collective-permute-start | bytes 43016 | tf_op jit(solution)/shard_map/ppermute | solution.py:371
  203.3 6.7 %collective-permute-done.22 = bf16[32,3584]{1,0:T(8,128)(2,1)S(1)} collective-permute-done((bf16[32,3584]{1,0:T(8,128)(2,1)S(1)}, bf16[32,3584]{1,0:T(8,128)(2,1)S(1)}, u32[]{:S(2)}, u32[]{:S(2)}) %collective-permute-start.22) | collective-permute-done | bytes 229408 | tf_op jit(solution)/shard_map/ppermute | solution.py:371
  (101 shorter events, 20.2 us)
Async XLA Ops:
  0.6 30.7 %copy-start.4 = (bf16[32,3584]{1,0:T(8,128)(2,1)S(1)}, bf16[32,3584]{1,0:T(8,128)(2,1)}, u32[]{:S(2)}) copy-start(bf16[32,3584]{1,0:T(8,128)(2,1)} %param.10) | copy-start | bytes 688132
  3.4 10.8 %collective-permute-start = (bf16[32,3712]{1,0:T(8,128)(2,1)S(1)}, bf16[32,3712]{1,0:T(8,128)(2,1)S(1)}, u32[]{:S(2)}, u32[]{:S(2)}) collective-permute-start(bf16[32,3712]{1,0:T(8,128)(2,1)S(1)} %pad_maximum_fusion.8), channel_id=1, source_target_pairs={{0,16},{1,17},{2,6},{3,7},{4,20},{5,21},{6,2},{7,3},{8,24},{9,25},... | collective-permute-start | bytes 712712 | tf_op jit(solution)/shard_map/ppermute | solution.py:371
  9.0 10.2 %collective-permute-start.10 = (f32[2,3584]{1,0:T(2,128)S(1)}, f32[2,3584]{1,0:T(2,128)S(1)}, u32[]{:S(2)}, u32[]{:S(2)}) collective-permute-start(f32[2,3584]{1,0:T(2,128)S(1)} %pad_maximum_fusion.9), channel_id=1, source_target_pairs={{0,1},{1,0},{2,3},{3,2},{4,5},{5,4},{6,7},{7,6},{8,9},{9,8},{10,11... | collective-permute-start | bytes 86024 | tf_op jit(solution)/shard_map/ppermute | solution.py:371
  15.1 16.2 %collective-permute-start.3 = (bf16[64,3712]{1,0:T(8,128)(2,1)S(1)}, bf16[64,3712]{1,0:T(8,128)(2,1)S(1)}, u32[]{:S(2)}, u32[]{:S(2)}) collective-permute-start(bf16[64,3712]{1,0:T(8,128)(2,1)S(1)} %pad_maximum_fusion.6), channel_id=1, source_target_pairs={{0,8},{1,9},{2,18},{3,19},{4,12},{5,13},{6,22},{7,23},{8,0},{9,1},... | collective-permute-start | bytes 1425416 | tf_op jit(solution)/shard_map/ppermute | solution.py:371
  16.2 17.4 %collective-permute-start.2 = (bf16[64,3712]{1,0:T(8,128)(2,1)S(1)}, bf16[64,3712]{1,0:T(8,128)(2,1)S(1)}, u32[]{:S(2)}, u32[]{:S(2)}) collective-permute-start(bf16[64,3712]{1,0:T(8,128)(2,1)S(1)} %pad_maximum_fusion.6), channel_id=1, source_target_pairs={{0,4},{1,5},{2,3},{3,2},{4,0},{5,1},{6,7},{7,6},{8,12},{9,13},{10,... | collective-permute-start | bytes 1425416 | tf_op jit(solution)/shard_map/ppermute | solution.py:371
  17.7 17.4 %collective-permute-start.1 = (bf16[64,3712]{1,0:T(8,128)(2,1)S(1)}, bf16[64,3712]{1,0:T(8,128)(2,1)S(1)}, u32[]{:S(2)}, u32[]{:S(2)}) collective-permute-start(bf16[64,3712]{1,0:T(8,128)(2,1)S(1)} %pad_maximum_fusion.6), channel_id=1, source_target_pairs={{0,1},{1,0},{2,10},{3,11},{4,5},{5,4},{6,14},{7,15},{8,9},{9,8},{1... | collective-permute-start | bytes 1425416 | tf_op jit(solution)/shard_map/ppermute | solution.py:371
  31.4 23.6 %collective-permute-start.8 = (bf16[128,3712]{1,0:T(8,128)(2,1)S(1)}, bf16[128,3712]{1,0:T(8,128)(2,1)S(1)}, u32[]{:S(2)}, u32[]{:S(2)}) collective-permute-start(bf16[128,3712]{1,0:T(8,128)(2,1)S(1)} %pad_maximum_fusion.4.refs_1_), channel_id=1, source_target_pairs={{0,2},{1,3},{2,0},{3,1},{4,6},{5,7},{6,4},{7,5},{8,10},{9,11},{10,... | collective-permute-start | bytes 2850824 | tf_op jit(solution)/shard_map/ppermute | solution.py:371
  31.5 8.7 %collective-permute-start.5 = (bf16[64,3712]{1,0:T(8,128)(2,1)S(1)}, bf16[64,3712]{1,0:T(8,128)(2,1)S(1)}, u32[]{:S(2)}, u32[]{:S(2)}) collective-permute-start(bf16[64,3712]{1,0:T(8,128)(2,1)S(1)} %collective-permute-done.3), channel_id=1, source_target_pairs={{0,4},{1,5},{2,3},{3,2},{4,0},{5,1},{6,7},{7,6},{8,12},{9,13},{10,... | collective-permute-start | bytes 1425416 | tf_op jit(solution)/shard_map/ppermute | solution.py:371
  33.1 11.7 %collective-permute-start.4 = (bf16[64,3712]{1,0:T(8,128)(2,1)S(1)}, bf16[64,3712]{1,0:T(8,128)(2,1)S(1)}, u32[]{:S(2)}, u32[]{:S(2)}) collective-permute-start(bf16[64,3712]{1,0:T(8,128)(2,1)S(1)} %collective-permute-done.3), channel_id=1, source_target_pairs={{0,1},{1,0},{2,10},{3,11},{4,5},{5,4},{6,14},{7,15},{8,9},{9,8},{1... | collective-permute-start | bytes 1425416 | tf_op jit(solution)/shard_map/ppermute | solution.py:371
  33.6 16.2 %collective-permute-start.6 = (bf16[64,3712]{1,0:T(8,128)(2,1)S(1)}, bf16[64,3712]{1,0:T(8,128)(2,1)S(1)}, u32[]{:S(2)}, u32[]{:S(2)}) collective-permute-start(bf16[64,3712]{1,0:T(8,128)(2,1)S(1)} %collective-permute-done.2), channel_id=1, source_target_pairs={{0,1},{1,0},{2,10},{3,11},{4,5},{5,4},{6,14},{7,15},{8,9},{9,8},{1... | collective-permute-start | bytes 1425416 | tf_op jit(solution)/shard_map/ppermute | solution.py:371
  44.9 10.1 %collective-permute-start.9 = (bf16[128,3712]{1,0:T(8,128)(2,1)S(1)}, bf16[128,3712]{1,0:T(8,128)(2,1)S(1)}, u32[]{:S(2)}, u32[]{:S(2)}) collective-permute-start(bf16[128,3712]{1,0:T(8,128)(2,1)S(1)} %pad_maximum_fusion.5.refs_2_), channel_id=1, source_target_pairs={{0,2},{1,3},{2,0},{3,1},{4,6},{5,7},{6,4},{7,5},{8,10},{9,11},{10,... | collective-permute-start | bytes 2850824 | tf_op jit(solution)/shard_map/ppermute | solution.py:371
  45.0 9.9 %collective-permute-start.7 = (bf16[64,3712]{1,0:T(8,128)(2,1)S(1)}, bf16[64,3712]{1,0:T(8,128)(2,1)S(1)}, u32[]{:S(2)}, u32[]{:S(2)}) collective-permute-start(bf16[64,3712]{1,0:T(8,128)(2,1)S(1)} %collective-permute-done.5), channel_id=1, source_target_pairs={{0,1},{1,0},{2,10},{3,11},{4,5},{5,4},{6,14},{7,15},{8,9},{9,8},{1... | collective-permute-start | bytes 1425416 | tf_op jit(solution)/shard_map/ppermute | solution.py:371
  46.0 35.7 %collective-permute-start.11 = (bf16[128,3712]{1,0:T(8,128)(2,1)S(1)}, bf16[128,3712]{1,0:T(8,128)(2,1)S(1)}, u32[]{:S(2)}, u32[]{:S(2)}) collective-permute-start(bf16[128,3712]{1,0:T(8,128)(2,1)S(1)} %pad_maximum_fusion.2.a), channel_id=1, source_target_pairs={{0,2},{1,3},{2,0},{3,1},{4,6},{5,7},{6,4},{7,5},{8,10},{9,11},{10,... | collective-permute-start | bytes 2850824 | tf_op jit(solution)/shard_map/ppermute | solution.py:371
  55.0 15.1 %copy-start.5 = (bf16[32,3584]{1,0:T(8,128)(2,1)S(1)}, bf16[32,3584]{1,0:T(8,128)(2,1)}, u32[]{:S(2)}) copy-start(bf16[32,3584]{1,0:T(8,128)(2,1)} %param.13) | copy-start | bytes 688132
  67.4 1.4 copy-start
  68.8 1.3 copy-start.1
  70.1 11.6 %collective-permute-start.12 = (bf16[128,3712]{1,0:T(8,128)(2,1)S(1)}, bf16[128,3712]{1,0:T(8,128)(2,1)S(1)}, u32[]{:S(2)}, u32[]{:S(2)}) collective-permute-start(bf16[128,3712]{1,0:T(8,128)(2,1)S(1)} %pad_maximum_fusion.3.b), channel_id=1, source_target_pairs={{0,2},{1,3},{2,0},{3,1},{4,6},{5,7},{6,4},{7,5},{8,10},{9,11},{10,... | collective-permute-start | bytes 2850824 | tf_op jit(solution)/shard_map/ppermute | solution.py:371
  70.1 8.9 %collective-permute-start.23 = (bf16[32,3584]{1,0:T(8,128)(2,1)S(1)}, bf16[32,3584]{1,0:T(8,128)(2,1)S(1)}, u32[]{:S(2)}, u32[]{:S(2)}) collective-permute-start(bf16[32,3584]{1,0:T(8,128)(2,1)S(1)} %copy-done.5), channel_id=1, source_target_pairs={{0,16},{1,17},{2,6},{3,7},{4,20},{5,21},{6,2},{7,3},{8,24},{9,25},... | collective-permute-start | bytes 688136 | tf_op jit(solution)/shard_map/ppermute | solution.py:371
  79.1 17.1 %collective-permute-start.24 = (bf16[64,3584]{1,0:T(8,128)(2,1)S(1)}, bf16[64,3584]{1,0:T(8,128)(2,1)S(1)}, u32[]{:S(2)}, u32[]{:S(2)}) collective-permute-start(bf16[64,3584]{1,0:T(8,128)(2,1)S(1)} %pad_maximum_fusion.7), channel_id=1, source_target_pairs={{0,8},{1,9},{2,18},{3,19},{4,12},{5,13},{6,22},{7,23},{8,0},{9,1},... | collective-permute-start | bytes 1376264 | tf_op jit(solution)/shard_map/ppermute | solution.py:371
  79.1 34.2 %collective-permute-start.26 = (bf16[64,3584]{1,0:T(8,128)(2,1)S(1)}, bf16[64,3584]{1,0:T(8,128)(2,1)S(1)}, u32[]{:S(2)}, u32[]{:S(2)}) collective-permute-start(bf16[64,3584]{1,0:T(8,128)(2,1)S(1)} %pad_maximum_fusion.7), channel_id=1, source_target_pairs={{0,1},{1,0},{2,10},{3,11},{4,5},{5,4},{6,14},{7,15},{8,9},{9,8},{1... | collective-permute-start | bytes 1376264 | tf_op jit(solution)/shard_map/ppermute | solution.py:371
  80.1 32.6 %collective-permute-start.25 = (bf16[64,3584]{1,0:T(8,128)(2,1)S(1)}, bf16[64,3584]{1,0:T(8,128)(2,1)S(1)}, u32[]{:S(2)}, u32[]{:S(2)}) collective-permute-start(bf16[64,3584]{1,0:T(8,128)(2,1)S(1)} %pad_maximum_fusion.7), channel_id=1, source_target_pairs={{0,4},{1,5},{2,3},{3,2},{4,0},{5,1},{6,7},{7,6},{8,12},{9,13},{10,... | collective-permute-start | bytes 1376264 | tf_op jit(solution)/shard_map/ppermute | solution.py:371
  96.1 9.7 %copy-start.2 = (f32[512,1024]{1,0:T(8,128)}, f32[512,1024]{1,0:T(8,128)S(1)}, u32[]{:S(2)}) copy-start(f32[512,1024]{1,0:T(8,128)S(1)} %get-tuple-element.46.up_pre) | copy-start | bytes 6291460
  96.1 19.4 %collective-permute-start.28 = (bf16[64,3584]{1,0:T(8,128)(2,1)S(1)}, bf16[64,3584]{1,0:T(8,128)(2,1)S(1)}, u32[]{:S(2)}, u32[]{:S(2)}) collective-permute-start(bf16[64,3584]{1,0:T(8,128)(2,1)S(1)} %collective-permute-done.24), channel_id=1, source_target_pairs={{0,1},{1,0},{2,10},{3,11},{4,5},{5,4},{6,14},{7,15},{8,9},{9,8},{1... | collective-permute-start | bytes 1376264 | tf_op jit(solution)/shard_map/ppermute | solution.py:371
  97.2 17.1 %collective-permute-start.27 = (bf16[64,3584]{1,0:T(8,128)(2,1)S(1)}, bf16[64,3584]{1,0:T(8,128)(2,1)S(1)}, u32[]{:S(2)}, u32[]{:S(2)}) collective-permute-start(bf16[64,3584]{1,0:T(8,128)(2,1)S(1)} %collective-permute-done.24), channel_id=1, source_target_pairs={{0,4},{1,5},{2,3},{3,2},{4,0},{5,1},{6,7},{7,6},{8,12},{9,13},{10,... | collective-permute-start | bytes 1376264 | tf_op jit(solution)/shard_map/ppermute | solution.py:371
  105.8 21.1 %collective-permute-start.14 = (bf16[256,3584]{1,0:T(8,128)(2,1)}, bf16[256,3584]{1,0:T(8,128)(2,1)}, u32[]{:S(2)}, u32[]{:S(2)}) collective-permute-start(bf16[256,3584]{1,0:T(8,128)(2,1)} %get-tuple-element.38), channel_id=1, source_target_pairs={{0,2},{1,3},{2,0},{3,1},{4,6},{5,7},{6,4},{7,5},{8,10},{9,11},{10,... | collective-permute-start | bytes 5505032 | tf_op jit(solution)/shard_map/ppermute | solution.py:371
  112.8 17.7 %collective-permute-start.13 = (bf16[256,3584]{1,0:T(8,128)(2,1)S(1)}, bf16[256,3584]{1,0:T(8,128)(2,1)S(1)}, u32[]{:S(2)}, u32[]{:S(2)}) collective-permute-start(bf16[256,3584]{1,0:T(8,128)(2,1)S(1)} %get-tuple-element.37), channel_id=1, source_target_pairs={{0,2},{1,3},{2,0},{3,1},{4,6},{5,7},{6,4},{7,5},{8,10},{9,11},{10,... | collective-permute-start | bytes 5505032 | tf_op jit(solution)/shard_map/ppermute | solution.py:371
  113.3 8.5 %collective-permute-start.30 = (bf16[64,3584]{1,0:T(8,128)(2,1)S(1)}, bf16[64,3584]{1,0:T(8,128)(2,1)S(1)}, u32[]{:S(2)}, u32[]{:S(2)}) collective-permute-start(bf16[64,3584]{1,0:T(8,128)(2,1)S(1)} %collective-permute-done.25), channel_id=1, source_target_pairs={{0,1},{1,0},{2,10},{3,11},{4,5},{5,4},{6,14},{7,15},{8,9},{9,8},{1... | collective-permute-start | bytes 1376264 | tf_op jit(solution)/shard_map/ppermute | solution.py:371
  114.3 12.4 %collective-permute-start.31 = (bf16[64,3584]{1,0:T(8,128)(2,1)S(1)}, bf16[64,3584]{1,0:T(8,128)(2,1)S(1)}, u32[]{:S(2)}, u32[]{:S(2)}) collective-permute-start(bf16[64,3584]{1,0:T(8,128)(2,1)S(1)} %collective-permute-done.27), channel_id=1, source_target_pairs={{0,1},{1,0},{2,10},{3,11},{4,5},{5,4},{6,14},{7,15},{8,9},{9,8},{1... | collective-permute-start | bytes 1376264 | tf_op jit(solution)/shard_map/ppermute | solution.py:371
  115.7 39.6 %collective-permute-start.29 = (bf16[256,3584]{1,0:T(8,128)(2,1)S(1)}, bf16[256,3584]{1,0:T(8,128)(2,1)S(1)}, u32[]{:S(2)}, u32[]{:S(2)}) collective-permute-start(bf16[256,3584]{1,0:T(8,128)(2,1)S(1)} %pad_maximum_fusion.near_own), channel_id=1, source_target_pairs={{0,2},{1,3},{2,0},{3,1},{4,6},{5,7},{6,4},{7,5},{8,10},{9,11},{10,... | collective-permute-start | bytes 5505032 | tf_op jit(solution)/shard_map/ppermute | solution.py:371
  126.8 28.4 %collective-permute-start.32 = (bf16[256,3584]{1,0:T(8,128)(2,1)S(1)}, bf16[256,3584]{1,0:T(8,128)(2,1)S(1)}, u32[]{:S(2)}, u32[]{:S(2)}) collective-permute-start(bf16[256,3584]{1,0:T(8,128)(2,1)S(1)} %pad_maximum_fusion.1.near_other), channel_id=1, source_target_pairs={{0,2},{1,3},{2,0},{3,1},{4,6},{5,7},{6,4},{7,5},{8,10},{9,11},{10,... | collective-permute-start | bytes 5505032 | tf_op jit(solution)/shard_map/ppermute | solution.py:371
  128.4 8.5 %collective-permute-start.16 = (bf16[64,3584]{1,0:T(8,128)(2,1)S(1)}, bf16[64,3584]{1,0:T(8,128)(2,1)S(1)}, u32[]{:S(2)}, u32[]{:S(2)}) collective-permute-start(bf16[64,3584]{1,0:T(8,128)(2,1)S(1)} %get-tuple-element.62), channel_id=1, source_target_pairs={{0,1},{1,0},{2,10},{3,11},{4,5},{5,4},{6,14},{7,15},{8,9},{9,8},{1... | collective-permute-start | bytes 1376264 | tf_op jit(solution)/shard_map/ppermute | solution.py:371
  129.4 12.5 %collective-permute-start.19 = (bf16[64,3584]{1,0:T(8,128)(2,1)S(1)}, bf16[64,3584]{1,0:T(8,128)(2,1)S(1)}, u32[]{:S(2)}, u32[]{:S(2)}) collective-permute-start(bf16[64,3584]{1,0:T(8,128)(2,1)S(1)} %get-tuple-element.63), channel_id=1, source_target_pairs={{0,1},{1,0},{2,10},{3,11},{4,5},{5,4},{6,14},{7,15},{8,9},{9,8},{1... | collective-permute-start | bytes 1376264 | tf_op jit(solution)/shard_map/ppermute | solution.py:371
  132.2 15.0 %collective-permute-start.18 = (bf16[64,3584]{1,0:T(8,128)(2,1)S(1)}, bf16[64,3584]{1,0:T(8,128)(2,1)S(1)}, u32[]{:S(2)}, u32[]{:S(2)}) collective-permute-start(bf16[64,3584]{1,0:T(8,128)(2,1)S(1)} %get-tuple-element.58), channel_id=1, source_target_pairs={{0,1},{1,0},{2,10},{3,11},{4,5},{5,4},{6,14},{7,15},{8,9},{9,8},{1... | collective-permute-start | bytes 1376264 | tf_op jit(solution)/shard_map/ppermute | solution.py:371
  143.8 8.5 %collective-permute-start.20 = (bf16[64,3584]{1,0:T(8,128)(2,1)S(1)}, bf16[64,3584]{1,0:T(8,128)(2,1)S(1)}, u32[]{:S(2)}, u32[]{:S(2)}) collective-permute-start(bf16[64,3584]{1,0:T(8,128)(2,1)S(1)} %get-tuple-element.60), channel_id=1, source_target_pairs={{0,4},{1,5},{2,3},{3,2},{4,0},{5,1},{6,7},{7,6},{8,12},{9,13},{10,... | collective-permute-start | bytes 1376264 | tf_op jit(solution)/shard_map/ppermute | solution.py:371
  145.7 52.4 %collective-permute-start.15 = (bf16[64,3584]{1,0:T(8,128)(2,1)S(1)}, bf16[64,3584]{1,0:T(8,128)(2,1)S(1)}, u32[]{:S(2)}, u32[]{:S(2)}) collective-permute-start(bf16[64,3584]{1,0:T(8,128)(2,1)S(1)} %get-tuple-element.57), channel_id=1, source_target_pairs={{0,1},{1,0},{2,10},{3,11},{4,5},{5,4},{6,14},{7,15},{8,9},{9,8},{1... | collective-permute-start | bytes 1376264 | tf_op jit(solution)/shard_map/ppermute | solution.py:371
  147.2 53.7 %collective-permute-start.17 = (bf16[64,3584]{1,0:T(8,128)(2,1)S(1)}, bf16[64,3584]{1,0:T(8,128)(2,1)S(1)}, u32[]{:S(2)}, u32[]{:S(2)}) collective-permute-start(bf16[64,3584]{1,0:T(8,128)(2,1)S(1)} %get-tuple-element.59), channel_id=1, source_target_pairs={{0,4},{1,5},{2,3},{3,2},{4,0},{5,1},{6,7},{7,6},{8,12},{9,13},{10,... | collective-permute-start | bytes 1376264 | tf_op jit(solution)/shard_map/ppermute | solution.py:371
  153.3 47.6 %collective-permute-start.21 = (bf16[64,3584]{1,0:T(8,128)(2,1)}, bf16[64,3584]{1,0:T(8,128)(2,1)S(1)}, u32[]{:S(2)}, u32[]{:S(2)}) collective-permute-start(bf16[64,3584]{1,0:T(8,128)(2,1)} %add_convert_fusion), channel_id=1, source_target_pairs={{0,8},{1,9},{2,18},{3,19},{4,12},{5,13},{6,22},{7,23},{8,0},{9,1},... | collective-permute-start | bytes 1376264 | tf_op jit(solution)/shard_map/ppermute | solution.py:371
  171.4 11.9 %copy-start.3 = (bf16[512,3584]{1,0:T(8,128)(2,1)S(1)}, bf16[512,3584]{1,0:T(8,128)(2,1)}, u32[]{:S(2)}) copy-start(bf16[512,3584]{1,0:T(8,128)(2,1)} %get-tuple-element.52) | copy-start | bytes 11010052
  182.3 3.8 %copy-start.7 = (bf16[3584]{0:T(1024)(128)(2,1)S(1)}, bf16[3584]{0:T(1024)(128)(2,1)}, u32[]{:S(2)}) copy-start(bf16[3584]{0:T(1024)(128)(2,1)} %param.12) | copy-start | bytes 21508
  182.3 3.8 %collective-permute-start.33 = (f32[3584]{0:T(1024)S(1)}, f32[3584]{0:T(1024)S(1)}, u32[]{:S(2)}, u32[]{:S(2)}) collective-permute-start(f32[3584]{0:T(1024)S(1)} %divide_subtract_fusion), channel_id=1, source_target_pairs={{0,1},{1,0},{2,3},{3,2},{4,5},{5,4},{6,7},{7,6},{8,9},{9,8},{10,11... | collective-permute-start | bytes 43016 | tf_op jit(solution)/shard_map/ppermute | solution.py:371
  183.3 26.7 %copy-start.6 = (f32[3584]{0:T(1024)S(1)}, f32[3584]{0:T(1024)}, u32[]{:S(2)}) copy-start(f32[3584]{0:T(1024)} %param.11) | copy-start | bytes 43012
  186.1 8.1 %collective-permute-start.36 = (f32[3584]{0:T(1024)S(1)}, f32[3584]{0:T(1024)S(1)}, u32[]{:S(2)}, u32[]{:S(2)}) collective-permute-start(f32[3584]{0:T(1024)S(1)} %add_add_fusion.2), channel_id=1, source_target_pairs={{0,6},{1,7},{2,4},{3,5},{4,2},{5,3},{6,0},{7,1},{8,14},{9,15},{10,... | collective-permute-start | bytes 43016 | tf_op jit(solution)/shard_map/ppermute | solution.py:371
  192.7 3.7 %collective-permute-start.35 = (f32[3584]{0:T(1024)S(1)}, f32[3584]{0:T(1024)S(1)}, u32[]{:S(2)}, u32[]{:S(2)}) collective-permute-start(f32[3584]{0:T(1024)S(1)} %add_add_fusion.2), channel_id=1, source_target_pairs={{0,4},{1,5},{2,6},{3,7},{4,0},{5,1},{6,2},{7,3},{8,12},{9,13},{10,... | collective-permute-start | bytes 43016 | tf_op jit(solution)/shard_map/ppermute | solution.py:371
  194.2 2.3 %collective-permute-start.34 = (f32[3584]{0:T(1024)S(1)}, f32[3584]{0:T(1024)S(1)}, u32[]{:S(2)}, u32[]{:S(2)}) collective-permute-start(f32[3584]{0:T(1024)S(1)} %add_add_fusion.2), channel_id=1, source_target_pairs={{0,2},{1,3},{2,0},{3,1},{4,6},{5,7},{6,4},{7,5},{8,10},{9,11},{10,... | collective-permute-start | bytes 43016 | tf_op jit(solution)/shard_map/ppermute | solution.py:371
  196.5 5.6 %collective-permute-start.39 = (f32[3584]{0:T(1024)S(1)}, f32[3584]{0:T(1024)S(1)}, u32[]{:S(2)}, u32[]{:S(2)}) collective-permute-start(f32[3584]{0:T(1024)S(1)} %add_add_fusion.1), channel_id=1, source_target_pairs={{0,24},{1,25},{2,26},{3,27},{4,28},{5,29},{6,30},{7,31},{8,16},{9,... | collective-permute-start | bytes 43016 | tf_op jit(solution)/shard_map/ppermute | solution.py:371
  196.6 5.4 %collective-permute-start.38 = (f32[3584]{0:T(1024)S(1)}, f32[3584]{0:T(1024)S(1)}, u32[]{:S(2)}, u32[]{:S(2)}) collective-permute-start(f32[3584]{0:T(1024)S(1)} %add_add_fusion.1), channel_id=1, source_target_pairs={{0,16},{1,17},{2,18},{3,19},{4,20},{5,21},{6,22},{7,23},{8,24},{9,... | collective-permute-start | bytes 43016 | tf_op jit(solution)/shard_map/ppermute | solution.py:371
  198.1 4.6 %collective-permute-start.37 = (f32[3584]{0:T(1024)S(1)}, f32[3584]{0:T(1024)S(1)}, u32[]{:S(2)}, u32[]{:S(2)}) collective-permute-start(f32[3584]{0:T(1024)S(1)} %add_add_fusion.1), channel_id=1, source_target_pairs={{0,8},{1,9},{2,10},{3,11},{4,12},{5,13},{6,14},{7,15},{8,0},{9,1},... | collective-permute-start | bytes 43016 | tf_op jit(solution)/shard_map/ppermute | solution.py:371
  201.1 8.9 %collective-permute-start.22 = (bf16[32,3584]{1,0:T(8,128)(2,1)S(1)}, bf16[32,3584]{1,0:T(8,128)(2,1)S(1)}, u32[]{:S(2)}, u32[]{:S(2)}) collective-permute-start(bf16[32,3584]{1,0:T(8,128)(2,1)S(1)} %add_convert_fusion.12), channel_id=1, source_target_pairs={{0,16},{1,17},{2,6},{3,7},{4,20},{5,21},{6,2},{7,3},{8,24},{9,25},... | collective-permute-start | bytes 688136 | tf_op jit(solution)/shard_map/ppermute | solution.py:371
where the time goes:
time: 211 us
  waiting for transfers between devices  78.8 us (37%)
  Pallas kernels  65.6 us (31%)
  starting transfers between devices  43.4 us (21%)
  other arithmetic  12.6 us (6%)
  local copies, waits for them, and re-layouts  6.1 us (3%)
  matrix products  3.22 us (2%)
    ppermute x40, waiting for transfers between devices, permute(): return lax.ppermute(value, BOTH, [(i, i ^ mask(i)) for i in range(devices)])  78.8 us
    pallas_call x6, Pallas kernels, call(): pl.pallas_call(kernel, in_specs=specs, out_specs=[VMEM] * len(outs), out_...  65.6 us
    ppermute x40, starting transfers between devices, permute(): return lax.ppermute(value, BOTH, [(i, i ^ mask(i)) for i in range(devices)])  43.4 us
    convert_element_type x4, other arithmetic, add(): return sum((a.astype(F32) for a in addends)).astype(BF16)  4.51 us
  transfers between devices with their start and end apart: 40, of which 19 were waited for; matrix products, arithmetic and copies ran while one was open for 7% of the time, Pallas kernels for 31%

commit v1 on v0

--- a/solution.py
+++ b/solution.py
@@ -115,8 +115,8 @@
 
 
 def fetches(source, buffer, sems, view, ahead=2):
-    count = buffer.shape[0]
-    copies = lambda i: pltpu.make_async_copy(view(source, i), buffer.at[i], sems.at[i])
+    count, slots = sems.shape[0], buffer.shape[0]
+    copies = lambda i: pltpu.make_async_copy(view(source, i), buffer.at[lax.rem(i, slots)], sems.at[i])
     for i in range(min(ahead, count)):
         copies(i).start()
 
@@ -143,12 +143,12 @@
     return fetches(gate_mat, gate_buf, gate_sems, view), fetches(up_mat, up_buf, up_sems, view)
 
 
-def own_kernel(experts, which, a, b, c, d, steer, gain, gate_mat, up_mat, gate_acc, up_acc, scaled, facts, gate_buf, up_buf, gate_sems, up_sems, squares):
+def own_kernel(experts, which, a, b, steer, gain, gate_mat, up_mat, gate_acc, up_acc, scaled, facts, gate_buf, up_buf, gate_sems, up_sems, squares):
     gate_wait, up_wait = half_fetches(gate_mat, up_mat, gate_buf, up_buf, gate_sems, up_sems, which[0])
     half, tile = scaled.shape[1], gate_buf.shape[2]
-    scale_rows((a, b, c, d), steer[which[0]], gain[which[0]], scaled, squares)
+    scale_rows((a, b), steer[which[0]], gain[which[0]], scaled, squares)
     first = 0
-    for source in (a, b, c, d):
+    for source in (a, b):
         rows = slice(first, first + source.shape[0])
         values = source[:, half:].astype(F32)
         lane = lax.broadcasted_iota(jnp.int32, values.shape, 1)
@@ -169,46 +169,48 @@
     lax.fori_loop(0, gate_buf.shape[0], step, 0)
 
 
-def other_kernel(which, a, b, c, d, steer, gain, gate_mat, up_mat, gate_acc, up_acc, facts, gate_pre, up_pre, activated, scaled, found, gate_buf, up_buf, gate_sems, up_sems, squares):
+def other_kernel(which, a, b, c, d, steer, gain, gate_mat, up_mat, *refs):
+    states, outs, scratch = (refs[0:3], refs[3:6]), (refs[6:11], refs[11:16]), refs[16:]
+    gate_buf, up_buf, gate_sems, up_sems, squares = scratch
     gate_wait, up_wait = half_fetches(gate_mat, up_mat, gate_buf, up_buf, gate_sems, up_sems, which[1])
-    half, tile = scaled.shape[1], gate_buf.shape[2]
-    scale_rows((a, b, c, d), steer[which[1]], gain[which[1]], scaled, squares)
-    old = facts[...]
-    total = column(old, SQUARES) + jnp.sum(squares[...], axis=1, keepdims=True)
-    found[...] = facts_of([column(old, WEIGHT), column(old, SIGNED), total, lax.rsqrt(total / (2 * half) + EPSILON)])
+    half, tile = a.shape[1] - 128, gate_buf.shape[2]
+    for blocks, state, out in zip(((a, b), (c, d)), states, outs):
+        scaled, found, old = out[3], out[4], state[2][...]
+        scale_rows(blocks, steer[which[1]], gain[which[1]], scaled, squares)
+        total = column(old, SQUARES) + jnp.sum(squares[...], axis=1, keepdims=True)
+        found[...] = facts_of([column(old, WEIGHT), column(old, SIGNED), total, lax.rsqrt(total / (2 * half) + EPSILON)])
 
     def step(i, carry):
         at = pl.ds(pl.multiple_of(i * tile, tile), tile)
-        inverse = column(found[...], INVERSE)
         gate_wait(i)
-        gate = (gate_acc[:, at] + split_dot(scaled, gate_buf[i])) * inverse
-        gate_pre[:, at] = gate
+        for (gate_acc, _, _), (gate_pre, _, _, scaled, found) in zip(states, outs):
+            gate = gate_acc[:, at] + jnp.dot(scaled[...], gate_buf[i], preferred_element_type=F32)
+            gate_pre[:, at] = gate * column(found[...], INVERSE)
         up_wait(i)
-        up = (up_acc[:, at] + split_dot(scaled, up_buf[i])) * inverse
-        up_pre[:, at] = up
-        activated[:, at] = (gate * jax.nn.sigmoid(gate) * up).astype(BF16)
+        for (_, up_acc, _), (gate_pre, up_pre, activated, scaled, found) in zip(states, outs):
+            up = up_acc[:, at] + jnp.dot(scaled[...], up_buf[i], preferred_element_type=F32)
+            up, gate = up * column(found[...], INVERSE), gate_pre[:, at]
+            up_pre[:, at] = up
+            activated[:, at] = (gate * jax.nn.sigmoid(gate) * up).astype(BF16)
         return carry
 
     lax.fori_loop(0, gate_buf.shape[0], step, 0)
 
 
-def half_products(which, blocks, steer, gain, gate_mat, up_mat, state=None):
+def half_products(which, blocks, steer, gain, gate_mat, up_mat, states=()):
     half, units = gate_mat.shape[1:]
-    rows, tile = sum(b.shape[0] for b in blocks), tile_of(units, 256)
-    unit, wide = ((rows, units), F32), ((rows, half), BF16)
-    facts = (rows, 128), F32
+    rows, tile = 2 * blocks[0].shape[0], tile_of(units, 256)
+    unit, wide, facts = ((rows, units), F32), ((rows, half), BF16), ((rows, 128), F32)
     buffer, sems = pltpu.VMEM((units // tile, half, tile), BF16), pltpu.SemaphoreType.DMA((units // tile,))
-    operands = [which, *blocks, steer, gain, gate_mat, up_mat]
-    specs = [SMEM] + [VMEM] * 6 + [ANY] * 2
-    if state is None:
+    operands = [which, *blocks, steer, gain, gate_mat, up_mat, *(v for state in states for v in state)]
+    specs = [SMEM] + [VMEM] * (len(blocks) + 2) + [ANY] * 2 + [VMEM] * (3 * len(states))
+    if states:
+        kernel = other_kernel
+        outs = [unit, unit, ((rows, units), BF16), wide, facts] * 2
+    else:
         experts = lax.axis_size("dp")
         kernel = lambda *refs: own_kernel(experts, *refs)
         outs = [unit, unit, wide, facts]
-    else:
-        kernel = other_kernel
-        operands += state
-        specs += [VMEM] * 3
-        outs = [unit, unit, ((rows, units), BF16), wide, facts]
     return call(
         kernel,
         operands,
@@ -216,53 +218,56 @@
         outs,
         [buffer, buffer, sems, sems, pltpu.VMEM((rows, 128), F32)],
         44,
-        4 * rows * half * units,
+        2 * len(blocks) * rows * half * units,
         4 * half * units,
     )
 
 
-def out_kernel(chosen, which, activated, facts, down_mat, near, far, buf, sems):
-    tile, height = buf.shape[2], near.shape[0]
-    tiles = buf.shape[0]
+def out_kernel(chosen, which, act_a, act_b, facts_a, facts_b, down_mat, near, far, buf, sems):
+    tiles, _, tile = buf.shape
+    height = act_a.shape[0] // 2
     start = which[chosen] * (tile * tiles)
-    wait = fetches(down_mat, buf, sems, lambda source, i: source.at[:, pl.ds(pl.multiple_of(start + i * tile, tile), tile)], 3)
+    take = fetches(down_mat, buf, sems, lambda source, i: source.at[:, pl.ds(pl.multiple_of(start + i * tile, tile), tile)], 3)
 
     def step(i, carry):
         at = pl.ds(pl.multiple_of(i * tile, tile), tile)
-        wait(i)
-        out = split_dot(activated, buf[i]) * column(facts[...], WEIGHT)
-        near[:, at] = out[:height].astype(BF16)
-        far[:, at] = out[height:].astype(BF16)
+        take(i)
+        for first, activated, facts in ((0, act_a, facts_a), (height, act_b, facts_b)):
+            out = jnp.dot(activated[...], buf[i], preferred_element_type=F32) * column(facts[...], WEIGHT)
+            near[first : first + height, at] = out[:height].astype(BF16)
+            far[first : first + height, at] = out[height:].astype(BF16)
         return carry
 
     lax.fori_loop(0, tiles, step, 0)
 
 
-def expert_out(chosen, which, activated, facts, down_mat):
-    rows, units = activated.shape
+def expert_out(chosen, which, acts, facts, down_mat):
+    rows, units = acts[0].shape
     half = down_mat.shape[1] // 2
     tile = tile_of(half, 512)
-    out = ((rows // 2, half), BF16)
+    out = ((rows, half), BF16)
     return call(
         lambda *refs: out_kernel(chosen, *refs),
-        (which, activated, facts, down_mat),
-        [SMEM, VMEM, VMEM, ANY],
+        (which, *acts, *facts, down_mat),
+        [SMEM] + [VMEM] * 4 + [ANY],
         [out, out],
         [pltpu.VMEM((half // tile, units, tile), BF16), pltpu.SemaphoreType.DMA((half // tile,))],
         44,
-        2 * rows * half * units,
+        4 * rows * half * units,
         2 * half * units,
     )
 
 
-def back_kernel(which, near_own, far_own, near_other, far_other, gate_pre, up_pre, facts, down_mat, gate_sum, up_sum, share, own_buf, other_buf, own_sems, other_sems):
+def back_kernel(which, near_own, far_own, near_other, far_other, gate_a, gate_b, up_a, up_b, facts_a, facts_b, down_mat, gate_sum, up_sum, share_a, share_b, own_buf, other_buf, own_sems, other_sems):
     tile, half = own_buf.shape[1:]
     view = lambda h: lambda source, i: source.at[pl.ds(i * tile, tile), pl.ds(pl.multiple_of(which[h] * half, half), half)]
     own_take = fetches(down_mat, own_buf, own_sems, view(0))
     other_take = fetches(down_mat, other_buf, other_sems, view(1))
     dims = (((1,), (1,)), ((), ()))
-    share[...] = jnp.zeros_like(share)
-    height = near_own.shape[0]
+    share_a[...] = jnp.zeros_like(share_a)
+    share_b[...] = jnp.zeros_like(share_b)
+    height = near_own.shape[0] // 2
+    groups = ((gate_a, up_a, facts_a, share_a), (gate_b, up_b, facts_b, share_b))
 
     def step(i, carry):
         at = pl.ds(pl.multiple_of(i * tile, tile), tile)
@@ -270,20 +275,21 @@
         other_take(i)
         gate_total, up_total = 0.0, 0.0
         for first, own, other in ((0, near_own, near_other), (height, far_own, far_other)):
+            product = lax.dot_general(own[...], own_buf[i], dims, preferred_element_type=F32)
+            product += lax.dot_general(other[...], other_buf[i], dims, preferred_element_type=F32)
             rows = slice(first, first + height)
-            known = facts[rows, :]
-            back = lax.dot_general(own[...], own_buf[i], dims, preferred_element_type=F32)
-            back += lax.dot_general(other[...], other_buf[i], dims, preferred_element_type=F32)
-            back *= column(known, SIGNED)
-            gate, up = gate_pre[rows, at], up_pre[rows, at]
-            sigma = jax.nn.sigmoid(gate)
-            grad_gate = back * up * sigma * (1.0 + gate * (1.0 - sigma))
-            grad_up = back * gate * sigma
-            inverse = column(known, INVERSE)
-            gate_total += jnp.sum(grad_gate * inverse, axis=0, keepdims=True)
-            up_total += jnp.sum(grad_up * inverse, axis=0, keepdims=True)
-            part = grad_gate * gate + grad_up * up
-            share[rows, :] += sum(part[:, c : c + 128] for c in range(0, tile, 128))
+            for number, (gate_pre, up_pre, facts, share) in enumerate(groups):
+                known = facts[rows, :]
+                back = product[number * height : (number + 1) * height] * column(known, SIGNED)
+                gate, up = gate_pre[rows, at], up_pre[rows, at]
+                sigma = jax.nn.sigmoid(gate)
+                grad_gate = back * up * sigma * (1.0 + gate * (1.0 - sigma))
+                grad_up = back * gate * sigma
+                inverse = column(known, INVERSE)
+                gate_total += jnp.sum(grad_gate * inverse, axis=0, keepdims=True)
+                up_total += jnp.sum(grad_up * inverse, axis=0, keepdims=True)
+                part = grad_gate * gate + grad_up * up
+                share[rows, :] += sum(part[:, c : c + 128] for c in range(0, tile, 128))
         gate_sum[:, at] = gate_total
         up_sum[:, at] = up_total
         return carry
@@ -293,23 +299,23 @@
 
 def expert_back(which, rows_of, down_mat, gate_pre, up_pre, facts):
     half = rows_of[0].shape[1]
-    rows, units = gate_pre.shape
+    rows, units = gate_pre[0].shape
     tile = tile_of(units, 256)
     buffer, sems = pltpu.VMEM((units // tile, tile, half), BF16), pltpu.SemaphoreType.DMA((units // tile,))
     return call(
         back_kernel,
-        (which, *rows_of, gate_pre, up_pre, facts, down_mat),
-        [SMEM] + [VMEM] * 7 + [ANY],
-        [((1, units), F32), ((1, units), F32), ((rows, 128), F32)],
+        (which, *rows_of, *gate_pre, *up_pre, *facts, down_mat),
+        [SMEM] + [VMEM] * 10 + [ANY],
+        [((1, units), F32), ((1, units), F32), ((rows, 128), F32), ((rows, 128), F32)],
         [buffer, buffer, sems, sems],
         44,
-        4 * rows * half * units,
+        8 * rows * half * units,
         4 * half * units,
     )
 
 
 def through_kernel(gate_sum, up_sum, gate_mat, up_mat, out, gate_buf, up_buf, gate_sems, up_sems):
-    tiles, tile, units = gate_buf.shape
+    slots, tile, units = gate_buf.shape
     view = lambda source, i: source.at[pl.ds(i * tile, tile), :]
     gate_wait = fetches(gate_mat, gate_buf, gate_sems, view)
     up_wait = fetches(up_mat, up_buf, up_sems, view)
@@ -318,32 +324,32 @@
     def step(i, carry):
         gate_wait(i)
         up_wait(i)
-
+        slot = lax.rem(i, slots)
         for r in range(tile // chunk):
             at = pl.ds(r * chunk, chunk)
             total = jnp.zeros((chunk, 128), F32)
             for c in range(0, units, 128):
                 lanes = slice(c, c + 128)
-                total += gate_buf[i, at, lanes].astype(F32) * gate_sum[:, lanes]
-                total += up_buf[i, at, lanes].astype(F32) * up_sum[:, lanes]
+                total += gate_buf[slot, at, lanes].astype(F32) * gate_sum[:, lanes]
+                total += up_buf[slot, at, lanes].astype(F32) * up_sum[:, lanes]
             to = pl.ds(pl.multiple_of(i * tile + r * chunk, chunk), chunk)
             out[:, to] = jnp.sum(total.T, axis=0, keepdims=True)
         return carry
 
-    lax.fori_loop(0, tiles, step, 0)
+    lax.fori_loop(0, gate_sems.shape[0], step, 0)
 
 
 def through_weights(gate_sum, up_sum, gate_mat, up_mat):
     full, units = gate_mat.shape
     tile = tile_of(full, 896)
-    buffer, sems = pltpu.VMEM((full // tile, tile, units), BF16), pltpu.SemaphoreType.DMA((full // tile,))
+    buffer, sems = pltpu.VMEM((4, tile, units), BF16), pltpu.SemaphoreType.DMA((full // tile,))
     return call(
         through_kernel,
         (gate_sum, up_sum, gate_mat, up_mat),
         [VMEM, VMEM, ANY, ANY],
         [((1, full), F32)],
         [buffer, buffer, sems, sems],
-        48,
+        44,
         512 * full * units,
         4 * full * units,
     )[0]
@@ -393,11 +399,12 @@
         p5 = hop(p1, last)
         p6 = hop(p2, last)
         p7 = hop(hold(p3, 3), last)
-        join = lambda a, b: jnp.concatenate([a, b], axis=0)
-        own_a = join(p0, p1)
-        own_b = join(jnp.where(even, p2, p4), jnp.where(even, p3, p5))
-        other_a = join(jnp.where(even, p4, p2), jnp.where(even, p5, p3))
-        return [own_a, own_b, other_a, join(p6, p7)], ((p3, p5), (p6, p7))
+        return p0, p1, p2, p3, p4, p5, p6, p7
+
+    def quarters(p):
+        own_b = jnp.where(even, p[2], p[4]), jnp.where(even, p[3], p[5])
+        other_a = jnp.where(even, p[4], p[2]), jnp.where(even, p[5], p[3])
+        return (p[0], p[1]), own_b, other_a, (p[6], p[7])
 
     gain = norm_gain.astype(F32)
     sign = (2 * contrast - 1).astype(F32)
@@ -410,20 +417,25 @@
     gain_halves = jnp.where(low_side, jnp.stack([vectors[1], vectors_other[1]]), jnp.stack([vectors_other[1], vectors[1]]))
     steer_halves, gain_halves = steer_halves[:, None, :], gain_halves[:, None, :]
 
-    (own_a, own_b, other_a, other_b), arrived = spread(jnp.concatenate([hidden, meta], axis=1))
+    pieces = spread(jnp.concatenate([hidden, meta], axis=1))
+    own_a, own_b, other_a, other_b = (jnp.concatenate(pair, axis=0) for pair in quarters(pieces))
     shared = (steer_halves, gain_halves, gate_halves, up_halves)
-    gate_acc, up_acc, own_scaled, facts = half_products(which, (own_a, own_b, swap(own_a), swap(own_b)), *shared)
-    other_far_a = swap(other_a)
-    other_b = after(other_b, facts)
-    gate_pre, up_pre, activated, other_scaled, facts = half_products(
-        which, (other_a, other_b, other_far_a, swap(other_b)), *shared, (gate_acc, up_acc, facts)
-    )
-    near_other, far_other = expert_out(1, which, activated, facts, down_mat)
+    state_a = half_products(which, (own_a, swap(own_a)), *shared)
+    far_other_a = swap(other_a)
+    state_b = half_products(which, (own_b, swap(own_b)), *shared)
+    split = lambda state: ((state[0], state[1], state[3]), state[2])
+    (state_a, own_scaled_a), (state_b, own_scaled_b) = split(state_a), split(state_b)
+    blocks = other_a, far_other_a, other_b, swap(other_b)
+    done = half_products(which, blocks, *shared, (state_a, state_b))
+    (gate_a, up_a, act_a, other_scaled_a, facts_a), (gate_b, up_b, act_b, other_scaled_b, facts_b) = done[:5], done[5:]
+    facts = facts_a, facts_b
+    near_other, far_other = expert_out(1, which, (act_a, act_b), facts, down_mat)
     here_other = swap(far_other)
-    near_own, far_own = expert_out(0, which, after(activated, near_other), facts, down_mat)
+    near_own, far_own = expert_out(0, which, (act_a, after(act_b, near_other)), facts, down_mat)
     here_own = swap(far_own)
 
-    targets, _ = spread(target, (*arrived, (activated,), (near_other,)))
+    gates = (pieces[3], pieces[5]), (pieces[6], pieces[7]), (act_b,), (near_other,)
+    targets = spread(target, gates)
 
     def add(*addends):
         return sum(a.astype(F32) for a in addends).astype(BF16)
@@ -432,6 +444,7 @@
     sum_own, sum_other = (near_own, here_own), (near_other, here_other)
     piece = lambda pair, i: add(*(v[i * rows : (i + 1) * rows] for v in pair))
     a7, a6 = piece(sum_other, 3), piece(sum_other, 2)
+    sum_own = near_own, after(here_own, a7, a6)
     a5 = jnp.where(even, piece(sum_other, 1), piece(sum_own, 3))
     a4 = jnp.where(even, piece(sum_other, 0), piece(sum_own, 2))
     a3 = jnp.where(even, piece(sum_own, 3), piece(sum_other, 1))
@@ -441,8 +454,16 @@
     b2 = hop(a6, last)
     b1 = hop(a5, last)
     b0 = hop(a4, last)
-    third1, third0 = add(a3, b3), add(a2, b2)
+    third1 = add(a3, b3)
     c1 = hop(third1, third)
+
+    own_a, own_b, other_a, other_b = quarters([after(v, a7, a6, a5, a4) for v in targets])
+    target_own = jnp.concatenate(own_a + own_b, axis=0)
+    target_other = jnp.concatenate(other_a + other_b, axis=0)
+    far = swap(target_own), swap(target_other)
+    rows_of = after(target_own, third1), far[0], target_other, far[1]
+    gate_sum, up_sum, share_a, share_b = expert_back(which, rows_of, down_mat, (gate_a, gate_b), (up_a, up_b), facts)
+    third0 = add(after(a2, gate_sum), b2)
     c0 = hop(third0, third)
     early = add(a1, b1, c1)
     d0 = hop(early, steps - 3)
@@ -452,16 +473,11 @@
         addends.append(hop(add(*(a[rows : 2 * rows] for a in addends)), step))
     out_tok = sum(a[:tokens].astype(F32) for a in addends)
     mixed = (hidden.astype(F32) + steering[None, :] + out_tok).astype(BF16)
-
-    own_a, own_b, other_a, other_b = targets
-    target_own = jnp.concatenate([own_a, own_b], axis=0)
-    target_other = jnp.concatenate([other_a, other_b], axis=0)
-    far = swap(target_own), swap(target_other)
-    rows_of = after(target_own, a7, a6, a5, a4), far[0], target_other, far[1]
-    gate_sum, up_sum, share = expert_back(which, rows_of, down_mat, gate_pre, up_pre, facts)
-    through = through_weights(after(gate_sum, third1, third0), up_sum, gate_mat, up_mat)[0]
-    along = jnp.sum(after(share, early), axis=1) * facts[:, INVERSE] * facts[:, INVERSE]
-    along_own, along_other = rows_times(along, own_scaled, 0), rows_times(along, other_scaled, 0)
+    through = through_weights(after(gate_sum, third0, early), up_sum, gate_mat, up_mat)[0]
+    weigh = lambda share, facts: jnp.sum(after(share, early), axis=1) * facts[:, INVERSE] * facts[:, INVERSE]
+    along_a, along_b = weigh(share_a, facts_a), weigh(share_b, facts_b)
+    along_own = rows_times(along_a, own_scaled_a, 0) + rows_times(along_b, own_scaled_b, 0)
+    along_other = rows_times(along_a, other_scaled_a, 0) + rows_times(along_b, other_scaled_b, 0)
     low_part, high_part = through[:half], through[half:]
     through_own = jnp.where(low_side, low_part, high_part)
     through_other = jnp.where(low_side, high_part, low_part)

time: 211 us -> 213 us (level)
  waiting for transfers between devices: 78.8 us -> 75.2 us
  local copies, waits for them, and re-layouts: 6.1 us -> 9.26 us
  Pallas kernels: 65.6 us -> 68.2 us
  starting transfers between devices: 43.4 us -> 40.9 us
  other arithmetic: 12.6 us -> 14.9 us
    ppermute x40, waiting for transfers between devices: 78.8 us -> 75.2 us  [permute(): return lax.ppermute(value, BOTH, [(i, i ^ mask(i)) for i in range(devices)])]
    unnamed x16 -> x29, local copies, waits for them, and re-layouts: 2.72 us -> 5.82 us
    pallas_call x6 -> x7, Pallas kernels: 65.6 us -> 68.2 us  [call(): pl.pallas_call(kernel, in_specs=specs, out_specs=[VMEM] * len(outs), out_...]
    ppermute x40, starting transfers between devices: 43.4 us -> 40.9 us  [permute(): return lax.ppermute(value, BOTH, [(i, i ^ mask(i)) for i in range(devices)])]
    convert_element_type x4 -> x5, other arithmetic: 4.51 us -> 6.19 us  [add(): return sum((a.astype(F32) for a in addends)).astype(BF16)]
  transfers between devices with their start and end apart: 40 -> 40, of which waited for: 19 -> 20; matrix products, arithmetic and copies ran while one was open for 7% -> 8% of each run, Pallas kernels for 31% -> 32%
where the time goes in v1:
time: 213 us; the launch traced here: 212 us
  waiting for transfers between devices  75.2 us (35%)
  Pallas kernels  68.2 us (32%)
  starting transfers between devices  40.9 us (19%)
  other arithmetic  14.9 us (7%)
  local copies, waits for them, and re-layouts  9.26 us (4%)
  matrix products  3.02 us (1%)
    ppermute x40, waiting for transfers between devices, permute(): return lax.ppermute(value, BOTH, [(i, i ^ mask(i)) for i in range(devices)])  75.2 us
    pallas_call x7, Pallas kernels, call(): pl.pallas_call(kernel, in_specs=specs, out_specs=[VMEM] * len(outs), out_...  68.2 us
    ppermute x40, starting transfers between devices, permute(): return lax.ppermute(value, BOTH, [(i, i ^ mask(i)) for i in range(devices)])  40.9 us
    convert_element_type x5, other arithmetic, add(): return sum((a.astype(F32) for a in addends)).astype(BF16)  6.19 us
    unnamed x29, local copies, waits for them, and re-layouts  5.82 us
  transfers between devices with their start and end apart: 40, of which 20 were waited for; matrix products, arithmetic and copies ran while one was open for 8% of the time, Pallas kernels for 32%

profile of v1, /device:TPU:0, one launch (start us, length us, event | category | flops | bytes accessed | tf_op | source)
XLA Modules:
  0.0 212.5 jit_solution(1402723872350915540)
XLA Ops:
  3.4 4.1 %collective-permute-start = (bf16[32,3712]{1,0:T(8,128)(2,1)S(1)}, bf16[32,3712]{1,0:T(8,128)(2,1)S(1)}, u32[]{:S(2)}, u32[]{:S(2)}) collective-permute-start(bf16[32,3712]{1,0:T(8,128)(2,1)S(1)} %pad_maximum_fusion.7), channel_id=1, source_target_pairs={{0,16},{1,17},{2,6},{3,7},{4,20},{5,21},{6,2},{7,3},{8,24},{9,25},... | collective-permute-start | bytes 712712 | tf_op jit(solution)/shard_map/ppermute | solution.py:377
  9.0 1.6 collective-permute-start.10
  12.1 2.1 collective-permute-done
  16.2 1.6 collective-permute-start.2
  17.8 1.5 collective-permute-start.1
  19.3 12.1 %collective-permute-done.3 = bf16[64,3712]{1,0:T(8,128)(2,1)S(1)} collective-permute-done((bf16[64,3712]{1,0:T(8,128)(2,1)S(1)}, bf16[64,3712]{1,0:T(8,128)(2,1)S(1)}, u32[]{:S(2)}, u32[]{:S(2)}) %collective-permute-start.3) | collective-permute-done | bytes 475168 | tf_op jit(solution)/shard_map/ppermute | solution.py:377
  31.6 1.6 collective-permute-start.5
  33.7 1.5 collective-permute-start.7
  35.3 5.0 %collective-permute-done.5 = bf16[64,3712]{1,0:T(8,128)(2,1)S(1)} collective-permute-done((bf16[64,3712]{1,0:T(8,128)(2,1)S(1)}, bf16[64,3712]{1,0:T(8,128)(2,1)S(1)}, u32[]{:S(2)}, u32[]{:S(2)}) %collective-permute-start.5) | collective-permute-done | bytes 475168 | tf_op jit(solution)/shard_map/ppermute | solution.py:377
  40.3 4.6 %collective-permute-done.4 = bf16[64,3712]{1,0:T(8,128)(2,1)S(1)} collective-permute-done((bf16[64,3712]{1,0:T(8,128)(2,1)S(1)}, bf16[64,3712]{1,0:T(8,128)(2,1)S(1)}, u32[]{:S(2)}, u32[]{:S(2)}) %collective-permute-start.4) | collective-permute-done | bytes 475168 | tf_op jit(solution)/shard_map/ppermute | solution.py:377
  46.1 3.8 %collective-permute-done.7 = bf16[64,3712]{1,0:T(8,128)(2,1)S(1)} collective-permute-done((bf16[64,3712]{1,0:T(8,128)(2,1)S(1)}, bf16[64,3712]{1,0:T(8,128)(2,1)S(1)}, u32[]{:S(2)}, u32[]{:S(2)}) %collective-permute-start.7) | collective-permute-done | bytes 475168 | tf_op jit(solution)/shard_map/ppermute | solution.py:377
  50.0 5.1 %collective-permute-done.8 = bf16[64,3712]{1,0:T(8,128)(2,1)S(1)} collective-permute-done((bf16[64,3712]{1,0:T(8,128)(2,1)S(1)}, bf16[64,3712]{1,0:T(8,128)(2,1)S(1)}, u32[]{:S(2)}, u32[]{:S(2)}) %collective-permute-start.8) | collective-permute-done | bytes 475168 | tf_op jit(solution)/shard_map/ppermute | solution.py:377
  55.8 7.3 %shard_map.113 = (f32[256,1024]{1,0:T(8,128)S(1)}, f32[256,1024]{1,0:T(8,128)S(1)}, bf16[256,3584]{1,0:T(8,128)(2,1)S(1)}, f32[256,128]{1,0:T(8,128)S(1)}) custom-call(s32[3]{0:T(128)S(1)} %pad_add_fusion.refs_0_.which, bf16[128,3712]{1,0:T(8,128)(2,1)S(1)} %pad_maximum_fusion.3.refs_1_, bf16[128,3712]{1,0:T(8,128)(2,1)S(1)} %collective-permute-done.11.refs_2_, ...), custom_call_target="tpu_custom_call" | custom-call | flops 3758096384 | bytes 14680064 | tf_op jit(solution)/shard_map/pallas_call | solution.py:71
  64.1 7.3 %shard_map.114 = (f32[256,1024]{1,0:T(8,128)S(1)}, f32[256,1024]{1,0:T(8,128)S(1)}, bf16[256,3584]{1,0:T(8,128)(2,1)S(1)}, f32[256,128]{1,0:T(8,128)S(1)}) custom-call(s32[3]{0:T(128)S(1)} %pad_add_fusion.refs_0_.which, bf16[128,3712]{1,0:T(8,128)(2,1)S(1)} %pad_maximum_fusion.4.refs_1_, bf16[128,3712]{1,0:T(8,128)(2,1)S(1)} %collective-permute-done.12.refs_2_, ...), custom_call_target="tpu_custom_call" | custom-call | flops 3758096384 | bytes 14680064 | tf_op jit(solution)/shard_map/pallas_call | solution.py:71
  71.5 1.3 copy-done
  74.7 15.5 %shard_map.115 = (f32[256,1024]{1,0:T(8,128)S(1)}, f32[256,1024]{1,0:T(8,128)S(1)}, bf16[256,1024]{1,0:T(8,128)(2,1)S(1)}, bf16[256,3584]{1,0:T(8,128)(2,1)}, f3...) custom-call(s32[3]{0:T(128)S(1)} %pad_add_fusion.refs_0_.which, ...), custom_call_target="tpu_custom_call" | custom-call | flops 7516192768 | bytes 14680064 | tf_op jit(solution)/shard_map/pallas_call | solution.py:71
  90.3 7.0 %shard_map.116 = (bf16[256,3584]{1,0:T(8,128)(2,1)S(1)}, bf16[256,3584]{1,0:T(8,128)(2,1)S(1)}) custom-call(s32[3]{0:T(128)S(1)} %pad_add_fusion.refs_0_.which, bf16[256,1024]{1,0:T(8,128)(2,1)S(1)} %get-tuple-element.54.refs_1_, bf16[256,1024]{1,0:T(8,128)(2,1)S(1)} %get-tuple-element.59.refs_2_, f32[256,128]{1,0:T(8,128)S(1)} %get-tuple-element.56.refs_3_.facts_a, ...), custom_call_target="tpu_custom_call" | custom-call | flops 3758096384 | bytes 7340032 | tf_op jit(solution)/shard_map/pallas_call | solution.py:71
  97.3 1.3 collective-permute-start.14
  98.6 1.4 collective-permute-start.17
  100.0 7.0 %shard_map.117 = (bf16[256,3584]{1,0:T(8,128)(2,1)S(1)}, bf16[256,3584]{1,0:T(8,128)(2,1)S(1)}) custom-call(s32[3]{0:T(128)S(1)} %pad_add_fusion.refs_0_.which, bf16[256,1024]{1,0:T(8,128)(2,1)S(1)} %get-tuple-element.54.refs_1_, bf16[256,1024]{1,0:T(8,128)(2,1)S(1)} %get-tuple-element.59.refs_2_, f32[256,128]{1,0:T(8,128)S(1)} %get-tuple-element.56.refs_3_.facts_a, ...), custom_call_target="tpu_custom_call" | custom-call | flops 3758096384 | bytes 7340032 | tf_op jit(solution)/shard_map/pallas_call | solution.py:71
  107.2 1.5 collective-permute-start.18
  108.7 3.3 %collective-permute-done.17 = bf16[64,3584]{1,0:T(8,128)(2,1)S(1)} collective-permute-done((bf16[64,3584]{1,0:T(8,128)(2,1)S(1)}, bf16[64,3584]{1,0:T(8,128)(2,1)S(1)}, u32[]{:S(2)}, u32[]{:S(2)}) %collective-permute-start.17) | collective-permute-done | bytes 458784 | tf_op jit(solution)/shard_map/ppermute | solution.py:377
  113.8 1.8 collective-permute-done.18
  116.6 4.0 %collective-permute-done.20 = bf16[64,3584]{1,0:T(8,128)(2,1)S(1)} collective-permute-done((bf16[64,3584]{1,0:T(8,128)(2,1)S(1)}, bf16[64,3584]{1,0:T(8,128)(2,1)S(1)}, u32[]{:S(2)}, u32[]{:S(2)}) %collective-permute-start.20) | collective-permute-done | bytes 458784 | tf_op jit(solution)/shard_map/ppermute | solution.py:377
  121.5 1.1 collective-permute-start.25
  124.5 1.3 broadcast_select_fusion.10
  125.9 3.9 %collective-permute-done.21 = bf16[64,3584]{1,0:T(8,128)(2,1)S(1)} collective-permute-done((bf16[64,3584]{1,0:T(8,128)(2,1)S(1)}, bf16[64,3584]{1,0:T(8,128)(2,1)S(1)}, u32[]{:S(2)}, u32[]{:S(2)}) %collective-permute-start.21) | collective-permute-done | bytes 458784 | tf_op jit(solution)/shard_map/ppermute | solution.py:377
  131.1 8.5 %collective-permute-done.25 = bf16[64,3584]{1,0:T(8,128)(2,1)S(1)} collective-permute-done((bf16[64,3584]{1,0:T(8,128)(2,1)S(1)}, bf16[64,3584]{1,0:T(8,128)(2,1)S(1)}, u32[]{:S(2)}, u32[]{:S(2)}) %collective-permute-start.25) | collective-permute-done | bytes 458784 | tf_op jit(solution)/shard_map/ppermute | solution.py:377
  139.8 4.7 %collective-permute-done.22 = bf16[64,3584]{1,0:T(8,128)(2,1)S(1)} collective-permute-done((bf16[64,3584]{1,0:T(8,128)(2,1)S(1)}, bf16[64,3584]{1,0:T(8,128)(2,1)S(1)}, u32[]{:S(2)}, u32[]{:S(2)}) %collective-permute-start.22) | collective-permute-done | bytes 458784 | tf_op jit(solution)/shard_map/ppermute | solution.py:377
  144.5 2.2 %add_convert_fusion.8 = (bf16[64,3584]{1,0:T(8,128)(2,1)}, bf16[64,3584]{1,0:T(8,128)(2,1)S(1)}) fusion(bf16[256,3584]{1,0:T(8,128)(2,1)S(1)} %collective-permute-done.13, bf16[256,3584]{1,0:T(8,128)(2,1)S(1)} %get-tuple-element.60, bf16[64,3584]{1,0:T(8,128)(2,1)S(1)} %collective-permute-done.22, bf16[256,3584]{1,0:T(8,128)(2,1)} %copy-done.7, ...), kind=kLoop, calls=%fused_computation.17 | loop fusion | flops 3899392 | bytes 4128769 | tf_op jit(solution)/shard_map/convert_element_type | solution.py:441
  146.8 1.5 collective-permute-start.30
  149.7 3.3 %collective-permute-done.29 = bf16[64,3584]{1,0:T(8,128)(2,1)S(1)} collective-permute-done((bf16[64,3584]{1,0:T(8,128)(2,1)S(1)}, bf16[64,3584]{1,0:T(8,128)(2,1)S(1)}, u32[]{:S(2)}, u32[]{:S(2)}) %collective-permute-start.29) | collective-permute-done | bytes 458784 | tf_op jit(solution)/shard_map/ppermute | solution.py:377
  154.0 1.2 collective-permute-done.30
  157.3 1.2 copy-done.13
  158.5 13.4 %shard_map.118 = (f32[1,1024]{1,0:T(1,128)S(1)}, f32[1,1024]{1,0:T(1,128)S(1)}, f32[256,128]{1,0:T(8,128)S(1)}, f32[256,128]{1,0:T(8,128)S(1)}) custom-call(s32[3]{0:T(128)S(1)} %pad_add_fusion.refs_0_.which, bf16[256,3584]{1,0:T(8,128)(2,1)S(1)} %pad_maximum_fusion.near_own, bf16[256,3584]{1,0:T(8,128)(2,1)S(1)} %collective-permute-done.23.far_own, ...), custom_call_target="tpu_custom_call" | custom-call | flops 7516192768 | bytes 14680064 | tf_op jit(solution)/shard_map/pallas_call | solution.py:71
  172.8 1.2 collective-permute-start.28
  174.3 2.0 convolution_reduce_fusion.1
  176.6 10.6 %shard_map.119 = f32[1,7168]{1,0:T(1,128)S(1)} custom-call(f32[1,1024]{1,0:T(1,128)S(1)} %get-tuple-element.84.gate_sum, f32[1,1024]{1,0:T(1,128)S(1)} %get-tuple-element.85.up_sum, bf16[7168,1024]{1,0:T(8,128)(2,1)} %bitcast.29, bf16[7168,1024]{1,0:T(8,128)(2,1)} %bitcast.33), custom_call_target="tpu_custom_call" | custom-call | flops 3758096384 | bytes 29360128 | tf_op jit(solution)/shard_map/pallas_call | solution.py:71
  189.1 2.1 collective-permute-done.33
  191.3 1.9 collective-permute-start.35
  193.3 1.2 collective-permute-done.36
  195.8 1.6 collective-permute-start.39
  197.4 1.2 collective-permute-start.38
  198.7 1.5 collective-permute-start.37
  200.2 1.1 add_convert_fusion.12
  201.3 1.1 collective-permute-start.32
  203.0 7.7 %collective-permute-done.32 = bf16[32,3584]{1,0:T(8,128)(2,1)S(1)} collective-permute-done((bf16[32,3584]{1,0:T(8,128)(2,1)S(1)}, bf16[32,3584]{1,0:T(8,128)(2,1)S(1)}, u32[]{:S(2)}, u32[]{:S(2)}) %collective-permute-start.32) | collective-permute-done | bytes 229408 | tf_op jit(solution)/shard_map/ppermute | solution.py:377
  210.7 1.8 add_convert_fusion.11
  (121 shorter events, 31.0 us)
Async XLA Ops:
  0.6 30.8 %copy-start.6 = (bf16[32,3584]{1,0:T(8,128)(2,1)S(1)}, bf16[32,3584]{1,0:T(8,128)(2,1)}, u32[]{:S(2)}) copy-start(bf16[32,3584]{1,0:T(8,128)(2,1)} %param.10) | copy-start | bytes 688132
  3.4 10.8 %collective-permute-start = (bf16[32,3712]{1,0:T(8,128)(2,1)S(1)}, bf16[32,3712]{1,0:T(8,128)(2,1)S(1)}, u32[]{:S(2)}, u32[]{:S(2)}) collective-permute-start(bf16[32,3712]{1,0:T(8,128)(2,1)S(1)} %pad_maximum_fusion.7), channel_id=1, source_target_pairs={{0,16},{1,17},{2,6},{3,7},{4,20},{5,21},{6,2},{7,3},{8,24},{9,25},... | collective-permute-start | bytes 712712 | tf_op jit(solution)/shard_map/ppermute | solution.py:377
  9.0 7.2 %collective-permute-start.10 = (f32[2,3584]{1,0:T(2,128)S(1)}, f32[2,3584]{1,0:T(2,128)S(1)}, u32[]{:S(2)}, u32[]{:S(2)}) collective-permute-start(f32[2,3584]{1,0:T(2,128)S(1)} %pad_maximum_fusion.8), channel_id=1, source_target_pairs={{0,1},{1,0},{2,3},{3,2},{4,5},{5,4},{6,7},{7,6},{8,9},{9,8},{10,11... | collective-permute-start | bytes 86024 | tf_op jit(solution)/shard_map/ppermute | solution.py:377
  15.1 16.3 %collective-permute-start.3 = (bf16[64,3712]{1,0:T(8,128)(2,1)S(1)}, bf16[64,3712]{1,0:T(8,128)(2,1)S(1)}, u32[]{:S(2)}, u32[]{:S(2)}) collective-permute-start(bf16[64,3712]{1,0:T(8,128)(2,1)S(1)} %pad_maximum_fusion.5), channel_id=1, source_target_pairs={{0,8},{1,9},{2,18},{3,19},{4,12},{5,13},{6,22},{7,23},{8,0},{9,1},... | collective-permute-start | bytes 1425416 | tf_op jit(solution)/shard_map/ppermute | solution.py:377
  16.2 17.5 %collective-permute-start.2 = (bf16[64,3712]{1,0:T(8,128)(2,1)S(1)}, bf16[64,3712]{1,0:T(8,128)(2,1)S(1)}, u32[]{:S(2)}, u32[]{:S(2)}) collective-permute-start(bf16[64,3712]{1,0:T(8,128)(2,1)S(1)} %pad_maximum_fusion.5), channel_id=1, source_target_pairs={{0,4},{1,5},{2,3},{3,2},{4,0},{5,1},{6,7},{7,6},{8,12},{9,13},{10,... | collective-permute-start | bytes 1425416 | tf_op jit(solution)/shard_map/ppermute | solution.py:377
  17.8 17.4 %collective-permute-start.1 = (bf16[64,3712]{1,0:T(8,128)(2,1)S(1)}, bf16[64,3712]{1,0:T(8,128)(2,1)S(1)}, u32[]{:S(2)}, u32[]{:S(2)}) collective-permute-start(bf16[64,3712]{1,0:T(8,128)(2,1)S(1)} %pad_maximum_fusion.5), channel_id=1, source_target_pairs={{0,1},{1,0},{2,10},{3,11},{4,5},{5,4},{6,14},{7,15},{8,9},{9,8},{1... | collective-permute-start | bytes 1425416 | tf_op jit(solution)/shard_map/ppermute | solution.py:377
  31.5 24.3 %collective-permute-start.11 = (bf16[128,3712]{1,0:T(8,128)(2,1)S(1)}, bf16[128,3712]{1,0:T(8,128)(2,1)S(1)}, u32[]{:S(2)}, u32[]{:S(2)}) collective-permute-start(bf16[128,3712]{1,0:T(8,128)(2,1)S(1)} %pad_maximum_fusion.3.refs_1_), channel_id=1, source_target_pairs={{0,2},{1,3},{2,0},{3,1},{4,6},{5,7},{6,4},{7,5},{8,10},{9,11},{10,... | collective-permute-start | bytes 2850824 | tf_op jit(solution)/shard_map/ppermute | solution.py:377
  31.6 8.7 %collective-permute-start.5 = (bf16[64,3712]{1,0:T(8,128)(2,1)S(1)}, bf16[64,3712]{1,0:T(8,128)(2,1)S(1)}, u32[]{:S(2)}, u32[]{:S(2)}) collective-permute-start(bf16[64,3712]{1,0:T(8,128)(2,1)S(1)} %collective-permute-done.3), channel_id=1, source_target_pairs={{0,4},{1,5},{2,3},{3,2},{4,0},{5,1},{6,7},{7,6},{8,12},{9,13},{10,... | collective-permute-start | bytes 1425416 | tf_op jit(solution)/shard_map/ppermute | solution.py:377
  33.2 11.7 %collective-permute-start.4 = (bf16[64,3712]{1,0:T(8,128)(2,1)S(1)}, bf16[64,3712]{1,0:T(8,128)(2,1)S(1)}, u32[]{:S(2)}, u32[]{:S(2)}) collective-permute-start(bf16[64,3712]{1,0:T(8,128)(2,1)S(1)} %collective-permute-done.3), channel_id=1, source_target_pairs={{0,1},{1,0},{2,10},{3,11},{4,5},{5,4},{6,14},{7,15},{8,9},{9,8},{1... | collective-permute-start | bytes 1425416 | tf_op jit(solution)/shard_map/ppermute | solution.py:377
  33.7 16.2 %collective-permute-start.7 = (bf16[64,3712]{1,0:T(8,128)(2,1)S(1)}, bf16[64,3712]{1,0:T(8,128)(2,1)S(1)}, u32[]{:S(2)}, u32[]{:S(2)}) collective-permute-start(bf16[64,3712]{1,0:T(8,128)(2,1)S(1)} %collective-permute-done.2), channel_id=1, source_target_pairs={{0,1},{1,0},{2,10},{3,11},{4,5},{5,4},{6,14},{7,15},{8,9},{9,8},{1... | collective-permute-start | bytes 1425416 | tf_op jit(solution)/shard_map/ppermute | solution.py:377
  45.0 29.7 %collective-permute-start.6 = (bf16[128,3712]{1,0:T(8,128)(2,1)S(1)}, bf16[128,3712]{1,0:T(8,128)(2,1)S(1)}, u32[]{:S(2)}, u32[]{:S(2)}) collective-permute-start(bf16[128,3712]{1,0:T(8,128)(2,1)S(1)} %pad_maximum_fusion.2.a), channel_id=1, source_target_pairs={{0,2},{1,3},{2,0},{3,1},{4,6},{5,7},{6,4},{7,5},{8,10},{9,11},{10,... | collective-permute-start | bytes 2850824 | tf_op jit(solution)/shard_map/ppermute | solution.py:377
  45.1 9.9 %collective-permute-start.8 = (bf16[64,3712]{1,0:T(8,128)(2,1)S(1)}, bf16[64,3712]{1,0:T(8,128)(2,1)S(1)}, u32[]{:S(2)}, u32[]{:S(2)}) collective-permute-start(bf16[64,3712]{1,0:T(8,128)(2,1)S(1)} %collective-permute-done.5), channel_id=1, source_target_pairs={{0,1},{1,0},{2,10},{3,11},{4,5},{5,4},{6,14},{7,15},{8,9},{9,8},{1... | collective-permute-start | bytes 1425416 | tf_op jit(solution)/shard_map/ppermute | solution.py:377
  46.0 9.2 %copy-start.10 = (bf16[32,3584]{1,0:T(8,128)(2,1)S(1)}, bf16[32,3584]{1,0:T(8,128)(2,1)}, u32[]{:S(2)}) copy-start(bf16[32,3584]{1,0:T(8,128)(2,1)} %param.13) | copy-start | bytes 688132
  46.1 18.1 %collective-permute-start.12 = (bf16[128,3712]{1,0:T(8,128)(2,1)S(1)}, bf16[128,3712]{1,0:T(8,128)(2,1)S(1)}, u32[]{:S(2)}, u32[]{:S(2)}) collective-permute-start(bf16[128,3712]{1,0:T(8,128)(2,1)S(1)} %pad_maximum_fusion.4.refs_1_), channel_id=1, source_target_pairs={{0,2},{1,3},{2,0},{3,1},{4,6},{5,7},{6,4},{7,5},{8,10},{9,11},{10,... | collective-permute-start | bytes 2850824 | tf_op jit(solution)/shard_map/ppermute | solution.py:377
  55.1 19.7 %collective-permute-start.9 = (bf16[128,3712]{1,0:T(8,128)(2,1)S(1)}, bf16[128,3712]{1,0:T(8,128)(2,1)S(1)}, u32[]{:S(2)}, u32[]{:S(2)}) collective-permute-start(bf16[128,3712]{1,0:T(8,128)(2,1)S(1)} %constant_dynamic-update-slice_fusion.c), channel_id=1, source_target_pairs={{0,2},{1,3},{2,0},{3,1},{4,6},{5,7},{6,4},{7,5},{8,10},{9,11},{10,... | collective-permute-start | bytes 2850824 | tf_op jit(solution)/shard_map/ppermute | solution.py:377
  55.2 43.4 %collective-permute-start.16 = (bf16[32,3584]{1,0:T(8,128)(2,1)S(1)}, bf16[32,3584]{1,0:T(8,128)(2,1)S(1)}, u32[]{:S(2)}, u32[]{:S(2)}) collective-permute-start(bf16[32,3584]{1,0:T(8,128)(2,1)S(1)} %copy-done.10), channel_id=1, source_target_pairs={{0,16},{1,17},{2,6},{3,7},{4,20},{5,21},{6,2},{7,3},{8,24},{9,25},... | collective-permute-start | bytes 688136 | tf_op jit(solution)/shard_map/ppermute | solution.py:377
  64.1 7.3 %copy-start.3 = (f32[256,1024]{1,0:T(8,128)}, f32[256,1024]{1,0:T(8,128)S(1)}, u32[]{:S(2)}) copy-start(f32[256,1024]{1,0:T(8,128)S(1)} %get-tuple-element.49.refs_1_) | copy-start | bytes 3145732
  97.3 24.2 %collective-permute-start.14 = (bf16[256,3584]{1,0:T(8,128)(2,1)S(1)}, bf16[256,3584]{1,0:T(8,128)(2,1)S(1)}, u32[]{:S(2)}, u32[]{:S(2)}) collective-permute-start(bf16[256,3584]{1,0:T(8,128)(2,1)S(1)} %get-tuple-element.62), channel_id=1, source_target_pairs={{0,2},{1,3},{2,0},{3,1},{4,6},{5,7},{6,4},{7,5},{8,10},{9,11},{10,... | collective-permute-start | bytes 5505032 | tf_op jit(solution)/shard_map/ppermute | solution.py:377
  98.6 13.4 %collective-permute-start.17 = (bf16[64,3584]{1,0:T(8,128)(2,1)S(1)}, bf16[64,3584]{1,0:T(8,128)(2,1)S(1)}, u32[]{:S(2)}, u32[]{:S(2)}) collective-permute-start(bf16[64,3584]{1,0:T(8,128)(2,1)S(1)} %pad_maximum_fusion.6), channel_id=1, source_target_pairs={{0,8},{1,9},{2,18},{3,19},{4,12},{5,13},{6,22},{7,23},{8,0},{9,1},... | collective-permute-start | bytes 1376264 | tf_op jit(solution)/shard_map/ppermute | solution.py:377
  107.0 16.6 %collective-permute-start.13 = (bf16[256,3584]{1,0:T(8,128)(2,1)S(1)}, bf16[256,3584]{1,0:T(8,128)(2,1)S(1)}, u32[]{:S(2)}, u32[]{:S(2)}) collective-permute-start(bf16[256,3584]{1,0:T(8,128)(2,1)S(1)} %get-tuple-element.61), channel_id=1, source_target_pairs={{0,2},{1,3},{2,0},{3,1},{4,6},{5,7},{6,4},{7,5},{8,10},{9,11},{10,... | collective-permute-start | bytes 5505032 | tf_op jit(solution)/shard_map/ppermute | solution.py:377
  107.2 8.5 %collective-permute-start.18 = (bf16[64,3584]{1,0:T(8,128)(2,1)S(1)}, bf16[64,3584]{1,0:T(8,128)(2,1)S(1)}, u32[]{:S(2)}, u32[]{:S(2)}) collective-permute-start(bf16[64,3584]{1,0:T(8,128)(2,1)S(1)} %pad_maximum_fusion.6), channel_id=1, source_target_pairs={{0,4},{1,5},{2,3},{3,2},{4,0},{5,1},{6,7},{7,6},{8,12},{9,13},{10,... | collective-permute-start | bytes 1376264 | tf_op jit(solution)/shard_map/ppermute | solution.py:377
  112.0 8.6 %collective-permute-start.20 = (bf16[64,3584]{1,0:T(8,128)(2,1)S(1)}, bf16[64,3584]{1,0:T(8,128)(2,1)S(1)}, u32[]{:S(2)}, u32[]{:S(2)}) collective-permute-start(bf16[64,3584]{1,0:T(8,128)(2,1)S(1)} %collective-permute-done.17), channel_id=1, source_target_pairs={{0,4},{1,5},{2,3},{3,2},{4,0},{5,1},{6,7},{7,6},{8,12},{9,13},{10,... | collective-permute-start | bytes 1376264 | tf_op jit(solution)/shard_map/ppermute | solution.py:377
  112.8 18.0 %collective-permute-start.19 = (bf16[64,3584]{1,0:T(8,128)(2,1)S(1)}, bf16[64,3584]{1,0:T(8,128)(2,1)S(1)}, u32[]{:S(2)}, u32[]{:S(2)}) collective-permute-start(bf16[64,3584]{1,0:T(8,128)(2,1)S(1)} %pad_maximum_fusion.6), channel_id=1, source_target_pairs={{0,1},{1,0},{2,10},{3,11},{4,5},{5,4},{6,14},{7,15},{8,9},{9,8},{1... | collective-permute-start | bytes 1376264 | tf_op jit(solution)/shard_map/ppermute | solution.py:377
  115.7 14.2 %collective-permute-start.21 = (bf16[64,3584]{1,0:T(8,128)(2,1)S(1)}, bf16[64,3584]{1,0:T(8,128)(2,1)S(1)}, u32[]{:S(2)}, u32[]{:S(2)}) collective-permute-start(bf16[64,3584]{1,0:T(8,128)(2,1)S(1)} %collective-permute-done.17), channel_id=1, source_target_pairs={{0,1},{1,0},{2,10},{3,11},{4,5},{5,4},{6,14},{7,15},{8,9},{9,8},{1... | collective-permute-start | bytes 1376264 | tf_op jit(solution)/shard_map/ppermute | solution.py:377
  120.6 19.1 %collective-permute-start.24 = (bf16[64,3584]{1,0:T(8,128)(2,1)S(1)}, bf16[64,3584]{1,0:T(8,128)(2,1)S(1)}, u32[]{:S(2)}, u32[]{:S(2)}) collective-permute-start(bf16[64,3584]{1,0:T(8,128)(2,1)S(1)} %collective-permute-done.18), channel_id=1, source_target_pairs={{0,1},{1,0},{2,10},{3,11},{4,5},{5,4},{6,14},{7,15},{8,9},{9,8},{1... | collective-permute-start | bytes 1376264 | tf_op jit(solution)/shard_map/ppermute | solution.py:377
  121.5 4.4 %copy-start.7 = (bf16[256,3584]{1,0:T(8,128)(2,1)}, bf16[256,3584]{1,0:T(8,128)(2,1)S(1)}, u32[]{:S(2)}) copy-start(bf16[256,3584]{1,0:T(8,128)(2,1)S(1)} %collective-permute-done.14) | copy-start | bytes 5505028
  121.5 18.1 %collective-permute-start.25 = (bf16[64,3584]{1,0:T(8,128)(2,1)S(1)}, bf16[64,3584]{1,0:T(8,128)(2,1)S(1)}, u32[]{:S(2)}, u32[]{:S(2)}) collective-permute-start(bf16[64,3584]{1,0:T(8,128)(2,1)S(1)} %collective-permute-done.20), channel_id=1, source_target_pairs={{0,1},{1,0},{2,10},{3,11},{4,5},{5,4},{6,14},{7,15},{8,9},{9,8},{1... | collective-permute-start | bytes 1376264 | tf_op jit(solution)/shard_map/ppermute | solution.py:377
  123.6 21.0 %collective-permute-start.22 = (bf16[64,3584]{1,0:T(8,128)(2,1)S(1)}, bf16[64,3584]{1,0:T(8,128)(2,1)S(1)}, u32[]{:S(2)}, u32[]{:S(2)}) collective-permute-start(bf16[64,3584]{1,0:T(8,128)(2,1)S(1)} %get-tuple-element.103), channel_id=1, source_target_pairs={{0,1},{1,0},{2,10},{3,11},{4,5},{5,4},{6,14},{7,15},{8,9},{9,8},{1... | collective-permute-start | bytes 1376264 | tf_op jit(solution)/shard_map/ppermute | solution.py:377
  129.8 23.2 %collective-permute-start.29 = (bf16[64,3584]{1,0:T(8,128)(2,1)S(1)}, bf16[64,3584]{1,0:T(8,128)(2,1)S(1)}, u32[]{:S(2)}, u32[]{:S(2)}) collective-permute-start(bf16[64,3584]{1,0:T(8,128)(2,1)S(1)} %get-tuple-element.99), channel_id=1, source_target_pairs={{0,1},{1,0},{2,10},{3,11},{4,5},{5,4},{6,14},{7,15},{8,9},{9,8},{1... | collective-permute-start | bytes 1376264 | tf_op jit(solution)/shard_map/ppermute | solution.py:377
  131.1 26.2 %collective-permute-start.23 = (bf16[256,3584]{1,0:T(8,128)(2,1)S(1)}, bf16[256,3584]{1,0:T(8,128)(2,1)S(1)}, u32[]{:S(2)}, u32[]{:S(2)}) collective-permute-start(bf16[256,3584]{1,0:T(8,128)(2,1)S(1)} %pad_maximum_fusion.near_own), channel_id=1, source_target_pairs={{0,2},{1,3},{2,0},{3,1},{4,6},{5,7},{6,4},{7,5},{8,10},{9,11},{10,... | collective-permute-start | bytes 5505032 | tf_op jit(solution)/shard_map/ppermute | solution.py:377
  139.8 17.5 %collective-permute-start.26 = (bf16[256,3584]{1,0:T(8,128)(2,1)S(1)}, bf16[256,3584]{1,0:T(8,128)(2,1)S(1)}, u32[]{:S(2)}, u32[]{:S(2)}) collective-permute-start(bf16[256,3584]{1,0:T(8,128)(2,1)S(1)} %pad_maximum_fusion.1.near_other), channel_id=1, source_target_pairs={{0,2},{1,3},{2,0},{3,1},{4,6},{5,7},{6,4},{7,5},{8,10},{9,11},{10,... | collective-permute-start | bytes 5505032 | tf_op jit(solution)/shard_map/ppermute | solution.py:377
  146.8 8.5 %collective-permute-start.30 = (bf16[64,3584]{1,0:T(8,128)(2,1)S(1)}, bf16[64,3584]{1,0:T(8,128)(2,1)S(1)}, u32[]{:S(2)}, u32[]{:S(2)}) collective-permute-start(bf16[64,3584]{1,0:T(8,128)(2,1)S(1)} %get-tuple-element.101), channel_id=1, source_target_pairs={{0,4},{1,5},{2,3},{3,2},{4,0},{5,1},{6,7},{7,6},{8,12},{9,13},{10,... | collective-permute-start | bytes 1376264 | tf_op jit(solution)/shard_map/ppermute | solution.py:377
  148.6 23.2 %collective-permute-start.27 = (bf16[64,3584]{1,0:T(8,128)(2,1)}, bf16[64,3584]{1,0:T(8,128)(2,1)S(1)}, u32[]{:S(2)}, u32[]{:S(2)}) collective-permute-start(bf16[64,3584]{1,0:T(8,128)(2,1)} %get-tuple-element.102), channel_id=1, source_target_pairs={{0,1},{1,0},{2,10},{3,11},{4,5},{5,4},{6,14},{7,15},{8,9},{9,8},{1... | collective-permute-start | bytes 1376264 | tf_op jit(solution)/shard_map/ppermute | solution.py:377
  153.0 45.7 %collective-permute-start.15 = (bf16[64,3584]{1,0:T(8,128)(2,1)}, bf16[64,3584]{1,0:T(8,128)(2,1)S(1)}, u32[]{:S(2)}, u32[]{:S(2)}) collective-permute-start(bf16[64,3584]{1,0:T(8,128)(2,1)} %get-tuple-element.97), channel_id=1, source_target_pairs={{0,1},{1,0},{2,10},{3,11},{4,5},{5,4},{6,14},{7,15},{8,9},{9,8},{1... | collective-permute-start | bytes 1376264 | tf_op jit(solution)/shard_map/ppermute | solution.py:377
  156.2 43.9 %collective-permute-start.31 = (bf16[64,3584]{1,0:T(8,128)(2,1)}, bf16[64,3584]{1,0:T(8,128)(2,1)}, u32[]{:S(2)}, u32[]{:S(2)}) collective-permute-start(bf16[64,3584]{1,0:T(8,128)(2,1)} %add_convert_fusion), channel_id=1, source_target_pairs={{0,8},{1,9},{2,18},{3,19},{4,12},{5,13},{6,22},{7,23},{8,0},{9,1},... | collective-permute-start | bytes 1376264 | tf_op jit(solution)/shard_map/ppermute | solution.py:377
  172.8 27.4 %collective-permute-start.28 = (bf16[64,3584]{1,0:T(8,128)(2,1)}, bf16[64,3584]{1,0:T(8,128)(2,1)S(1)}, u32[]{:S(2)}, u32[]{:S(2)}) collective-permute-start(bf16[64,3584]{1,0:T(8,128)(2,1)} %add_convert_fusion.2), channel_id=1, source_target_pairs={{0,4},{1,5},{2,3},{3,2},{4,0},{5,1},{6,7},{7,6},{8,12},{9,13},{10,... | collective-permute-start | bytes 1376264 | tf_op jit(solution)/shard_map/ppermute | solution.py:377
  174.2 2.1 copy-start.9
  187.4 3.8 %collective-permute-start.33 = (f32[3584]{0:T(1024)S(1)}, f32[3584]{0:T(1024)S(1)}, u32[]{:S(2)}, u32[]{:S(2)}) collective-permute-start(f32[3584]{0:T(1024)S(1)} %divide_subtract_fusion), channel_id=1, source_target_pairs={{0,1},{1,0},{2,3},{3,2},{4,5},{5,4},{6,7},{7,6},{8,9},{9,8},{10,11... | collective-permute-start | bytes 43016 | tf_op jit(solution)/shard_map/ppermute | solution.py:377
  188.1 3.1 %copy-start.12 = (bf16[3584]{0:T(1024)(128)(2,1)S(1)}, bf16[3584]{0:T(1024)(128)(2,1)}, u32[]{:S(2)}) copy-start(bf16[3584]{0:T(1024)(128)(2,1)} %param.12) | copy-start | bytes 21508
  188.1 12.1 %copy-start.8 = (bf16[64,3584]{1,0:T(8,128)(2,1)S(1)}, bf16[64,3584]{1,0:T(8,128)(2,1)}, u32[]{:S(2)}) copy-start(bf16[64,3584]{1,0:T(8,128)(2,1)} %get-tuple-element.100) | copy-start | bytes 1376260
  188.5 22.2 %copy-start.11 = (f32[3584]{0:T(1024)S(1)}, f32[3584]{0:T(1024)}, u32[]{:S(2)}) copy-start(f32[3584]{0:T(1024)} %param.11) | copy-start | bytes 43012
  191.2 3.2 %collective-permute-start.36 = (f32[3584]{0:T(1024)S(1)}, f32[3584]{0:T(1024)S(1)}, u32[]{:S(2)}, u32[]{:S(2)}) collective-permute-start(f32[3584]{0:T(1024)S(1)} %add_add_fusion.2), channel_id=1, source_target_pairs={{0,6},{1,7},{2,4},{3,5},{4,2},{5,3},{6,0},{7,1},{8,14},{9,15},{10,... | collective-permute-start | bytes 43016 | tf_op jit(solution)/shard_map/ppermute | solution.py:377
  191.3 4.0 %collective-permute-start.35 = (f32[3584]{0:T(1024)S(1)}, f32[3584]{0:T(1024)S(1)}, u32[]{:S(2)}, u32[]{:S(2)}) collective-permute-start(f32[3584]{0:T(1024)S(1)} %add_add_fusion.2), channel_id=1, source_target_pairs={{0,4},{1,5},{2,6},{3,7},{4,0},{5,1},{6,2},{7,3},{8,12},{9,13},{10,... | collective-permute-start | bytes 43016 | tf_op jit(solution)/shard_map/ppermute | solution.py:377
  194.4 1.3 collective-permute-start.34
  195.8 6.6 %collective-permute-start.39 = (f32[3584]{0:T(1024)S(1)}, f32[3584]{0:T(1024)S(1)}, u32[]{:S(2)}, u32[]{:S(2)}) collective-permute-start(f32[3584]{0:T(1024)S(1)} %add_add_fusion.1), channel_id=1, source_target_pairs={{0,24},{1,25},{2,26},{3,27},{4,28},{5,29},{6,30},{7,31},{8,16},{9,... | collective-permute-start | bytes 43016 | tf_op jit(solution)/shard_map/ppermute | solution.py:377
  197.4 4.9 %collective-permute-start.38 = (f32[3584]{0:T(1024)S(1)}, f32[3584]{0:T(1024)S(1)}, u32[]{:S(2)}, u32[]{:S(2)}) collective-permute-start(f32[3584]{0:T(1024)S(1)} %add_add_fusion.1), channel_id=1, source_target_pairs={{0,16},{1,17},{2,18},{3,19},{4,20},{5,21},{6,22},{7,23},{8,24},{9,... | collective-permute-start | bytes 43016 | tf_op jit(solution)/shard_map/ppermute | solution.py:377
  198.7 3.7 %collective-permute-start.37 = (f32[3584]{0:T(1024)S(1)}, f32[3584]{0:T(1024)S(1)}, u32[]{:S(2)}, u32[]{:S(2)}) collective-permute-start(f32[3584]{0:T(1024)S(1)} %add_add_fusion.1), channel_id=1, source_target_pairs={{0,8},{1,9},{2,10},{3,11},{4,12},{5,13},{6,14},{7,15},{8,0},{9,1},... | collective-permute-start | bytes 43016 | tf_op jit(solution)/shard_map/ppermute | solution.py:377
  201.3 9.4 %collective-permute-start.32 = (bf16[32,3584]{1,0:T(8,128)(2,1)S(1)}, bf16[32,3584]{1,0:T(8,128)(2,1)S(1)}, u32[]{:S(2)}, u32[]{:S(2)}) collective-permute-start(bf16[32,3584]{1,0:T(8,128)(2,1)S(1)} %add_convert_fusion.12), channel_id=1, source_target_pairs={{0,16},{1,17},{2,6},{3,7},{4,20},{5,21},{6,2},{7,3},{8,24},{9,25},... | collective-permute-start | bytes 688136 | tf_op jit(solution)/shard_map/ppermute | solution.py:377
  (6 other events, 7.0 us)

commit v2 on v1

--- a/solution.py
+++ b/solution.py
@@ -217,7 +217,7 @@
         specs,
         outs,
         [buffer, buffer, sems, sems, pltpu.VMEM((rows, 128), F32)],
-        44,
+        35,
         2 * len(blocks) * rows * half * units,
         4 * half * units,
     )
@@ -252,7 +252,7 @@
         [SMEM] + [VMEM] * 4 + [ANY],
         [out, out],
         [pltpu.VMEM((half // tile, units, tile), BF16), pltpu.SemaphoreType.DMA((half // tile,))],
-        44,
+        37,
         4 * rows * half * units,
         2 * half * units,
     )
@@ -308,7 +308,7 @@
         [SMEM] + [VMEM] * 10 + [ANY],
         [((1, units), F32), ((1, units), F32), ((rows, 128), F32), ((rows, 128), F32)],
         [buffer, buffer, sems, sems],
-        44,
+        37,
         8 * rows * half * units,
         4 * half * units,
     )
@@ -349,7 +349,7 @@
         [VMEM, VMEM, ANY, ANY],
         [((1, full), F32)],
         [buffer, buffer, sems, sems],
-        44,
+        40,
         512 * full * units,
         4 * full * units,
     )[0]

time: 213 us -> 205 us (0.962)
  Pallas kernels: 68.2 us -> 63.5 us
  waiting for transfers between devices: 75.2 us -> 78.9 us
  local copies, waits for them, and re-layouts: 9.26 us -> 5.97 us
  other arithmetic: 14.9 us -> 12.5 us
    pallas_call x7, Pallas kernels: 68.2 us -> 63.5 us  [call(): pl.pallas_call(kernel, in_specs=specs, out_specs=[VMEM] * len(outs), out_...]
    ppermute x40, waiting for transfers between devices: 75.2 us -> 78.9 us  [permute(): return lax.ppermute(value, BOTH, [(i, i ^ mask(i)) for i in range(devices)])]
    unnamed x29 -> x19, local copies, waits for them, and re-layouts: 5.82 us -> 2.54 us
    convert_element_type x5, other arithmetic: 6.19 us -> 3.67 us  [add(): return sum((a.astype(F32) for a in addends)).astype(BF16)]
  transfers between devices with their start and end apart: 40 -> 40, of which waited for: 20 -> 18; matrix products, arithmetic and copies ran while one was open for 8% -> 7% of each run, Pallas kernels for 32% -> 31%
where the time goes in v2:
time: 205 us
  waiting for transfers between devices  78.9 us (38%)
  Pallas kernels  63.5 us (31%)
  starting transfers between devices  39.8 us (19%)
  other arithmetic  12.5 us (6%)
  local copies, waits for them, and re-layouts  5.97 us (3%)
  matrix products  3.02 us (1%)
    ppermute x40, waiting for transfers between devices, permute(): return lax.ppermute(value, BOTH, [(i, i ^ mask(i)) for i in range(devices)])  78.9 us
    pallas_call x7, Pallas kernels, call(): pl.pallas_call(kernel, in_specs=specs, out_specs=[VMEM] * len(outs), out_...  63.5 us
    ppermute x40, starting transfers between devices, permute(): return lax.ppermute(value, BOTH, [(i, i ^ mask(i)) for i in range(devices)])  39.8 us
  transfers between devices with their start and end apart: 40, of which 18 were waited for; matrix products, arithmetic and copies ran while one was open for 7% of the time, Pallas kernels for 31%

profile of v2, /device:TPU:0, one launch (start us, length us, event | category | flops | bytes accessed | tf_op | source)
XLA Modules:
  0.0 204.8 jit_solution(4711909250407997248)
XLA Ops:
  3.4 4.1 %collective-permute-start = (bf16[32,3712]{1,0:T(8,128)(2,1)S(1)}, bf16[32,3712]{1,0:T(8,128)(2,1)S(1)}, u32[]{:S(2)}, u32[]{:S(2)}) collective-permute-start(bf16[32,3712]{1,0:T(8,128)(2,1)S(1)} %pad_maximum_fusion.7), channel_id=1, source_target_pairs={{0,16},{1,17},{2,6},{3,7},{4,20},{5,21},{6,2},{7,3},{8,24},{9,25},... | collective-permute-start | bytes 712712 | tf_op jit(solution)/shard_map/ppermute | solution.py:377
  9.0 1.6 collective-permute-start.10
  12.1 2.1 %collective-permute-done = bf16[32,3712]{1,0:T(8,128)(2,1)S(1)} collective-permute-done((bf16[32,3712]{1,0:T(8,128)(2,1)S(1)}, bf16[32,3712]{1,0:T(8,128)(2,1)S(1)}, u32[]{:S(2)}, u32[]{:S(2)}) %collective-permute-start) | collective-permute-done | bytes 237600 | tf_op jit(solution)/shard_map/ppermute | solution.py:377
  15.1 1.1 collective-permute-start.3
  16.2 1.6 collective-permute-start.2
  17.8 1.5 collective-permute-start.1
  19.3 12.1 %collective-permute-done.3 = bf16[64,3712]{1,0:T(8,128)(2,1)S(1)} collective-permute-done((bf16[64,3712]{1,0:T(8,128)(2,1)S(1)}, bf16[64,3712]{1,0:T(8,128)(2,1)S(1)}, u32[]{:S(2)}, u32[]{:S(2)}) %collective-permute-start.3) | collective-permute-done | bytes 475168 | tf_op jit(solution)/shard_map/ppermute | solution.py:377
  31.6 1.6 collective-permute-start.5
  33.7 1.5 collective-permute-start.7
  35.3 5.0 %collective-permute-done.5 = bf16[64,3712]{1,0:T(8,128)(2,1)S(1)} collective-permute-done((bf16[64,3712]{1,0:T(8,128)(2,1)S(1)}, bf16[64,3712]{1,0:T(8,128)(2,1)S(1)}, u32[]{:S(2)}, u32[]{:S(2)}) %collective-permute-start.5) | collective-permute-done | bytes 475168 | tf_op jit(solution)/shard_map/ppermute | solution.py:377
  40.3 4.6 %collective-permute-done.4 = bf16[64,3712]{1,0:T(8,128)(2,1)S(1)} collective-permute-done((bf16[64,3712]{1,0:T(8,128)(2,1)S(1)}, bf16[64,3712]{1,0:T(8,128)(2,1)S(1)}, u32[]{:S(2)}, u32[]{:S(2)}) %collective-permute-start.4) | collective-permute-done | bytes 475168 | tf_op jit(solution)/shard_map/ppermute | solution.py:377
  46.1 3.8 %collective-permute-done.7 = bf16[64,3712]{1,0:T(8,128)(2,1)S(1)} collective-permute-done((bf16[64,3712]{1,0:T(8,128)(2,1)S(1)}, bf16[64,3712]{1,0:T(8,128)(2,1)S(1)}, u32[]{:S(2)}, u32[]{:S(2)}) %collective-permute-start.7) | collective-permute-done | bytes 475168 | tf_op jit(solution)/shard_map/ppermute | solution.py:377
  50.0 5.1 %collective-permute-done.8 = bf16[64,3712]{1,0:T(8,128)(2,1)S(1)} collective-permute-done((bf16[64,3712]{1,0:T(8,128)(2,1)S(1)}, bf16[64,3712]{1,0:T(8,128)(2,1)S(1)}, u32[]{:S(2)}, u32[]{:S(2)}) %collective-permute-start.8) | collective-permute-done | bytes 475168 | tf_op jit(solution)/shard_map/ppermute | solution.py:377
  55.8 7.3 %shard_map.113 = (f32[256,1024]{1,0:T(8,128)S(1)}, f32[256,1024]{1,0:T(8,128)S(1)}, bf16[256,3584]{1,0:T(8,128)(2,1)S(1)}, f32[256,128]{1,0:T(8,128)S(1)}) custom-call(s32[3]{0:T(128)S(1)} %pad_add_fusion.refs_0_.which, bf16[128,3712]{1,0:T(8,128)(2,1)S(1)} %pad_maximum_fusion.3.refs_1_, bf16[128,3712]{1,0:T(8,128)(2,1)S(1)} %collective-permute-done.11.refs_2_, ...), custom_call_target="tpu_custom_call" | custom-call | flops 3758096384 | bytes 14680064 | tf_op jit(solution)/shard_map/pallas_call | solution.py:71
  63.2 7.3 %shard_map.114 = (f32[256,1024]{1,0:T(8,128)S(1)}, f32[256,1024]{1,0:T(8,128)S(1)}, bf16[256,3584]{1,0:T(8,128)(2,1)S(1)}, f32[256,128]{1,0:T(8,128)S(1)}) custom-call(s32[3]{0:T(128)S(1)} %pad_add_fusion.refs_0_.which, bf16[128,3712]{1,0:T(8,128)(2,1)S(1)} %pad_maximum_fusion.4.refs_1_, bf16[128,3712]{1,0:T(8,128)(2,1)S(1)} %collective-permute-done.12.refs_2_, ...), custom_call_target="tpu_custom_call" | custom-call | flops 3758096384 | bytes 14680064 | tf_op jit(solution)/shard_map/pallas_call | solution.py:71
  70.5 1.2 copy-done
  71.7 12.1 %shard_map.115 = (f32[256,1024]{1,0:T(8,128)S(1)}, f32[256,1024]{1,0:T(8,128)S(1)}, bf16[256,1024]{1,0:T(8,128)(2,1)S(1)}, bf16[256,3584]{1,0:T(8,128)(2,1)S(1)}...) custom-call(s32[3]{0:T(128)S(1)} %pad_add_fusion.refs_0_.which, ...), custom_call_target="tpu_custom_call" | custom-call | flops 7516192768 | bytes 14680064 | tf_op jit(solution)/shard_map/pallas_call | solution.py:71
  83.8 1.2 copy-done.4
  85.0 6.9 %shard_map.116 = (bf16[256,3584]{1,0:T(8,128)(2,1)S(1)}, bf16[256,3584]{1,0:T(8,128)(2,1)S(1)}) custom-call(s32[3]{0:T(128)S(1)} %pad_add_fusion.refs_0_.which, bf16[256,1024]{1,0:T(8,128)(2,1)S(1)} %get-tuple-element.54.refs_1_, bf16[256,1024]{1,0:T(8,128)(2,1)S(1)} %get-tuple-element.59.refs_2_, f32[256,128]{1,0:T(8,128)S(1)} %get-tuple-element.56.refs_3_.facts_a, ...), custom_call_target="tpu_custom_call" | custom-call | flops 3758096384 | bytes 7340032 | tf_op jit(solution)/shard_map/pallas_call | solution.py:71
  92.0 1.2 collective-permute-start.14
  93.3 1.4 collective-permute-start.17
  94.6 6.8 %shard_map.117 = (bf16[256,3584]{1,0:T(8,128)(2,1)S(1)}, bf16[256,3584]{1,0:T(8,128)(2,1)S(1)}) custom-call(s32[3]{0:T(128)S(1)} %pad_add_fusion.refs_0_.which, bf16[256,1024]{1,0:T(8,128)(2,1)S(1)} %get-tuple-element.54.refs_1_, bf16[256,1024]{1,0:T(8,128)(2,1)S(1)} %get-tuple-element.59.refs_2_, f32[256,128]{1,0:T(8,128)S(1)} %get-tuple-element.56.refs_3_.facts_a, ...), custom_call_target="tpu_custom_call" | custom-call | flops 3758096384 | bytes 7340032 | tf_op jit(solution)/shard_map/pallas_call | solution.py:71
  101.7 1.5 collective-permute-start.18
  103.2 3.5 %collective-permute-done.17 = bf16[64,3584]{1,0:T(8,128)(2,1)S(1)} collective-permute-done((bf16[64,3584]{1,0:T(8,128)(2,1)S(1)}, bf16[64,3584]{1,0:T(8,128)(2,1)S(1)}, u32[]{:S(2)}, u32[]{:S(2)}) %collective-permute-start.17) | collective-permute-done | bytes 458784 | tf_op jit(solution)/shard_map/ppermute | solution.py:377
  108.5 1.7 collective-permute-done.18
  111.1 4.1 %collective-permute-done.20 = bf16[64,3584]{1,0:T(8,128)(2,1)S(1)} collective-permute-done((bf16[64,3584]{1,0:T(8,128)(2,1)S(1)}, bf16[64,3584]{1,0:T(8,128)(2,1)S(1)}, u32[]{:S(2)}, u32[]{:S(2)}) %collective-permute-start.20) | collective-permute-done | bytes 458784 | tf_op jit(solution)/shard_map/ppermute | solution.py:377
  116.0 1.2 collective-permute-start.25
  118.3 1.3 broadcast_select_fusion.10
  119.6 4.7 %collective-permute-done.21 = bf16[64,3584]{1,0:T(8,128)(2,1)S(1)} collective-permute-done((bf16[64,3584]{1,0:T(8,128)(2,1)S(1)}, bf16[64,3584]{1,0:T(8,128)(2,1)S(1)}, u32[]{:S(2)}, u32[]{:S(2)}) %collective-permute-start.21) | collective-permute-done | bytes 458784 | tf_op jit(solution)/shard_map/ppermute | solution.py:377
  125.7 8.5 %collective-permute-done.25 = bf16[64,3584]{1,0:T(8,128)(2,1)S(1)} collective-permute-done((bf16[64,3584]{1,0:T(8,128)(2,1)S(1)}, bf16[64,3584]{1,0:T(8,128)(2,1)S(1)}, u32[]{:S(2)}, u32[]{:S(2)}) %collective-permute-start.25) | collective-permute-done | bytes 458784 | tf_op jit(solution)/shard_map/ppermute | solution.py:377
  134.3 5.2 %collective-permute-done.22 = bf16[64,3584]{1,0:T(8,128)(2,1)S(1)} collective-permute-done((bf16[64,3584]{1,0:T(8,128)(2,1)S(1)}, bf16[64,3584]{1,0:T(8,128)(2,1)S(1)}, u32[]{:S(2)}, u32[]{:S(2)}) %collective-permute-start.22) | collective-permute-done | bytes 458784 | tf_op jit(solution)/shard_map/ppermute | solution.py:377
  140.0 1.3 collective-permute-start.30
  142.4 6.4 %collective-permute-done.29 = bf16[64,3584]{1,0:T(8,128)(2,1)S(1)} collective-permute-done((bf16[64,3584]{1,0:T(8,128)(2,1)S(1)}, bf16[64,3584]{1,0:T(8,128)(2,1)S(1)}, u32[]{:S(2)}, u32[]{:S(2)}) %collective-permute-start.29) | collective-permute-done | bytes 458784 | tf_op jit(solution)/shard_map/ppermute | solution.py:377
  150.9 1.0 collective-permute-start.31
  151.9 12.4 %shard_map.118 = (f32[1,1024]{1,0:T(1,128)S(1)}, f32[1,1024]{1,0:T(1,128)S(1)}, f32[256,128]{1,0:T(8,128)S(1)}, f32[256,128]{1,0:T(8,128)S(1)}) custom-call(s32[3]{0:T(128)S(1)} %pad_add_fusion.refs_0_.which, bf16[256,3584]{1,0:T(8,128)(2,1)S(1)} %pad_maximum_fusion.near_own, bf16[256,3584]{1,0:T(8,128)(2,1)S(1)} %collective-permute-done.23.far_own, ...), custom_call_target="tpu_custom_call" | custom-call | flops 7516192768 | bytes 14680064 | tf_op jit(solution)/shard_map/pallas_call | solution.py:71
  166.5 2.0 convolution_reduce_fusion.1
  168.8 10.6 %shard_map.119 = f32[1,7168]{1,0:T(1,128)S(1)} custom-call(f32[1,1024]{1,0:T(1,128)S(1)} %get-tuple-element.84.gate_sum, f32[1,1024]{1,0:T(1,128)S(1)} %get-tuple-element.85.up_sum, bf16[7168,1024]{1,0:T(8,128)(2,1)} %bitcast.29, bf16[7168,1024]{1,0:T(8,128)(2,1)} %bitcast.33), custom_call_target="tpu_custom_call" | custom-call | flops 3758096384 | bytes 29360128 | tf_op jit(solution)/shard_map/pallas_call | solution.py:71
  179.6 1.5 collective-permute-start.33
  181.8 1.6 collective-permute-done.33
  183.5 1.1 collective-permute-start.35
  184.6 2.0 collective-permute-done.36
  187.8 1.7 collective-permute-start.39
  189.5 1.2 collective-permute-start.38
  190.8 1.5 collective-permute-start.37
  192.2 1.2 add_convert_fusion.12
  193.4 1.4 collective-permute-start.32
  195.5 7.4 %collective-permute-done.32 = bf16[32,3584]{1,0:T(8,128)(2,1)S(1)} collective-permute-done((bf16[32,3584]{1,0:T(8,128)(2,1)S(1)}, bf16[32,3584]{1,0:T(8,128)(2,1)S(1)}, u32[]{:S(2)}, u32[]{:S(2)}) %collective-permute-start.32) | collective-permute-done | bytes 229408 | tf_op jit(solution)/shard_map/ppermute | solution.py:377
  202.9 1.9 add_convert_fusion.11
  (111 shorter events, 24.8 us)
Async XLA Ops:
  0.6 30.8 %copy-start.5 = (bf16[32,3584]{1,0:T(8,128)(2,1)S(1)}, bf16[32,3584]{1,0:T(8,128)(2,1)}, u32[]{:S(2)}) copy-start(bf16[32,3584]{1,0:T(8,128)(2,1)} %param.10) | copy-start | bytes 688132
  3.4 10.8 %collective-permute-start = (bf16[32,3712]{1,0:T(8,128)(2,1)S(1)}, bf16[32,3712]{1,0:T(8,128)(2,1)S(1)}, u32[]{:S(2)}, u32[]{:S(2)}) collective-permute-start(bf16[32,3712]{1,0:T(8,128)(2,1)S(1)} %pad_maximum_fusion.7), channel_id=1, source_target_pairs={{0,16},{1,17},{2,6},{3,7},{4,20},{5,21},{6,2},{7,3},{8,24},{9,25},... | collective-permute-start | bytes 712712 | tf_op jit(solution)/shard_map/ppermute | solution.py:377
  9.0 7.2 %collective-permute-start.10 = (f32[2,3584]{1,0:T(2,128)S(1)}, f32[2,3584]{1,0:T(2,128)S(1)}, u32[]{:S(2)}, u32[]{:S(2)}) collective-permute-start(f32[2,3584]{1,0:T(2,128)S(1)} %pad_maximum_fusion.8), channel_id=1, source_target_pairs={{0,1},{1,0},{2,3},{3,2},{4,5},{5,4},{6,7},{7,6},{8,9},{9,8},{10,11... | collective-permute-start | bytes 86024 | tf_op jit(solution)/shard_map/ppermute | solution.py:377
  15.1 16.3 %collective-permute-start.3 = (bf16[64,3712]{1,0:T(8,128)(2,1)S(1)}, bf16[64,3712]{1,0:T(8,128)(2,1)S(1)}, u32[]{:S(2)}, u32[]{:S(2)}) collective-permute-start(bf16[64,3712]{1,0:T(8,128)(2,1)S(1)} %pad_maximum_fusion.5), channel_id=1, source_target_pairs={{0,8},{1,9},{2,18},{3,19},{4,12},{5,13},{6,22},{7,23},{8,0},{9,1},... | collective-permute-start | bytes 1425416 | tf_op jit(solution)/shard_map/ppermute | solution.py:377
  16.2 17.5 %collective-permute-start.2 = (bf16[64,3712]{1,0:T(8,128)(2,1)S(1)}, bf16[64,3712]{1,0:T(8,128)(2,1)S(1)}, u32[]{:S(2)}, u32[]{:S(2)}) collective-permute-start(bf16[64,3712]{1,0:T(8,128)(2,1)S(1)} %pad_maximum_fusion.5), channel_id=1, source_target_pairs={{0,4},{1,5},{2,3},{3,2},{4,0},{5,1},{6,7},{7,6},{8,12},{9,13},{10,... | collective-permute-start | bytes 1425416 | tf_op jit(solution)/shard_map/ppermute | solution.py:377
  17.8 17.4 %collective-permute-start.1 = (bf16[64,3712]{1,0:T(8,128)(2,1)S(1)}, bf16[64,3712]{1,0:T(8,128)(2,1)S(1)}, u32[]{:S(2)}, u32[]{:S(2)}) collective-permute-start(bf16[64,3712]{1,0:T(8,128)(2,1)S(1)} %pad_maximum_fusion.5), channel_id=1, source_target_pairs={{0,1},{1,0},{2,10},{3,11},{4,5},{5,4},{6,14},{7,15},{8,9},{9,8},{1... | collective-permute-start | bytes 1425416 | tf_op jit(solution)/shard_map/ppermute | solution.py:377
  31.5 24.3 %collective-permute-start.11 = (bf16[128,3712]{1,0:T(8,128)(2,1)S(1)}, bf16[128,3712]{1,0:T(8,128)(2,1)S(1)}, u32[]{:S(2)}, u32[]{:S(2)}) collective-permute-start(bf16[128,3712]{1,0:T(8,128)(2,1)S(1)} %pad_maximum_fusion.3.refs_1_), channel_id=1, source_target_pairs={{0,2},{1,3},{2,0},{3,1},{4,6},{5,7},{6,4},{7,5},{8,10},{9,11},{10,... | collective-permute-start | bytes 2850824 | tf_op jit(solution)/shard_map/ppermute | solution.py:377
  31.6 8.7 %collective-permute-start.5 = (bf16[64,3712]{1,0:T(8,128)(2,1)S(1)}, bf16[64,3712]{1,0:T(8,128)(2,1)S(1)}, u32[]{:S(2)}, u32[]{:S(2)}) collective-permute-start(bf16[64,3712]{1,0:T(8,128)(2,1)S(1)} %collective-permute-done.3), channel_id=1, source_target_pairs={{0,4},{1,5},{2,3},{3,2},{4,0},{5,1},{6,7},{7,6},{8,12},{9,13},{10,... | collective-permute-start | bytes 1425416 | tf_op jit(solution)/shard_map/ppermute | solution.py:377
  33.2 11.7 %collective-permute-start.4 = (bf16[64,3712]{1,0:T(8,128)(2,1)S(1)}, bf16[64,3712]{1,0:T(8,128)(2,1)S(1)}, u32[]{:S(2)}, u32[]{:S(2)}) collective-permute-start(bf16[64,3712]{1,0:T(8,128)(2,1)S(1)} %collective-permute-done.3), channel_id=1, source_target_pairs={{0,1},{1,0},{2,10},{3,11},{4,5},{5,4},{6,14},{7,15},{8,9},{9,8},{1... | collective-permute-start | bytes 1425416 | tf_op jit(solution)/shard_map/ppermute | solution.py:377
  33.7 16.2 %collective-permute-start.7 = (bf16[64,3712]{1,0:T(8,128)(2,1)S(1)}, bf16[64,3712]{1,0:T(8,128)(2,1)S(1)}, u32[]{:S(2)}, u32[]{:S(2)}) collective-permute-start(bf16[64,3712]{1,0:T(8,128)(2,1)S(1)} %collective-permute-done.2), channel_id=1, source_target_pairs={{0,1},{1,0},{2,10},{3,11},{4,5},{5,4},{6,14},{7,15},{8,9},{9,8},{1... | collective-permute-start | bytes 1425416 | tf_op jit(solution)/shard_map/ppermute | solution.py:377
  45.0 26.7 %collective-permute-start.6 = (bf16[128,3712]{1,0:T(8,128)(2,1)S(1)}, bf16[128,3712]{1,0:T(8,128)(2,1)S(1)}, u32[]{:S(2)}, u32[]{:S(2)}) collective-permute-start(bf16[128,3712]{1,0:T(8,128)(2,1)S(1)} %pad_maximum_fusion.2.a), channel_id=1, source_target_pairs={{0,2},{1,3},{2,0},{3,1},{4,6},{5,7},{6,4},{7,5},{8,10},{9,11},{10,... | collective-permute-start | bytes 2850824 | tf_op jit(solution)/shard_map/ppermute | solution.py:377
  45.1 9.9 %collective-permute-start.8 = (bf16[64,3712]{1,0:T(8,128)(2,1)S(1)}, bf16[64,3712]{1,0:T(8,128)(2,1)S(1)}, u32[]{:S(2)}, u32[]{:S(2)}) collective-permute-start(bf16[64,3712]{1,0:T(8,128)(2,1)S(1)} %collective-permute-done.5), channel_id=1, source_target_pairs={{0,1},{1,0},{2,10},{3,11},{4,5},{5,4},{6,14},{7,15},{8,9},{9,8},{1... | collective-permute-start | bytes 1425416 | tf_op jit(solution)/shard_map/ppermute | solution.py:377
  46.0 9.2 %copy-start.6 = (bf16[32,3584]{1,0:T(8,128)(2,1)S(1)}, bf16[32,3584]{1,0:T(8,128)(2,1)}, u32[]{:S(2)}) copy-start(bf16[32,3584]{1,0:T(8,128)(2,1)} %param.13) | copy-start | bytes 688132
  46.1 17.1 %collective-permute-start.12 = (bf16[128,3712]{1,0:T(8,128)(2,1)S(1)}, bf16[128,3712]{1,0:T(8,128)(2,1)S(1)}, u32[]{:S(2)}, u32[]{:S(2)}) collective-permute-start(bf16[128,3712]{1,0:T(8,128)(2,1)S(1)} %pad_maximum_fusion.4.refs_1_), channel_id=1, source_target_pairs={{0,2},{1,3},{2,0},{3,1},{4,6},{5,7},{6,4},{7,5},{8,10},{9,11},{10,... | collective-permute-start | bytes 2850824 | tf_op jit(solution)/shard_map/ppermute | solution.py:377
  55.1 16.7 %collective-permute-start.9 = (bf16[128,3712]{1,0:T(8,128)(2,1)S(1)}, bf16[128,3712]{1,0:T(8,128)(2,1)S(1)}, u32[]{:S(2)}, u32[]{:S(2)}) collective-permute-start(bf16[128,3712]{1,0:T(8,128)(2,1)S(1)} %constant_dynamic-update-slice_fusion.c), channel_id=1, source_target_pairs={{0,2},{1,3},{2,0},{3,1},{4,6},{5,7},{6,4},{7,5},{8,10},{9,11},{10,... | collective-permute-start | bytes 2850824 | tf_op jit(solution)/shard_map/ppermute | solution.py:377
  55.2 38.0 %collective-permute-start.16 = (bf16[32,3584]{1,0:T(8,128)(2,1)S(1)}, bf16[32,3584]{1,0:T(8,128)(2,1)S(1)}, u32[]{:S(2)}, u32[]{:S(2)}) collective-permute-start(bf16[32,3584]{1,0:T(8,128)(2,1)S(1)} %copy-done.6), channel_id=1, source_target_pairs={{0,16},{1,17},{2,6},{3,7},{4,20},{5,21},{6,2},{7,3},{8,24},{9,25},... | collective-permute-start | bytes 688136 | tf_op jit(solution)/shard_map/ppermute | solution.py:377
  70.5 1.2 copy-start
  85.0 6.9 %copy-start.2 = (bf16[256,3584]{1,0:T(8,128)(2,1)}, bf16[256,3584]{1,0:T(8,128)(2,1)S(1)}, u32[]{:S(2)}) copy-start(bf16[256,3584]{1,0:T(8,128)(2,1)S(1)} %get-tuple-element.93) | copy-start | bytes 5505028
  92.0 24.0 %collective-permute-start.14 = (bf16[256,3584]{1,0:T(8,128)(2,1)S(1)}, bf16[256,3584]{1,0:T(8,128)(2,1)S(1)}, u32[]{:S(2)}, u32[]{:S(2)}) collective-permute-start(bf16[256,3584]{1,0:T(8,128)(2,1)S(1)} %get-tuple-element.62), channel_id=1, source_target_pairs={{0,2},{1,3},{2,0},{3,1},{4,6},{5,7},{6,4},{7,5},{8,10},{9,11},{10,... | collective-permute-start | bytes 5505032 | tf_op jit(solution)/shard_map/ppermute | solution.py:377
  93.3 13.4 %collective-permute-start.17 = (bf16[64,3584]{1,0:T(8,128)(2,1)S(1)}, bf16[64,3584]{1,0:T(8,128)(2,1)S(1)}, u32[]{:S(2)}, u32[]{:S(2)}) collective-permute-start(bf16[64,3584]{1,0:T(8,128)(2,1)S(1)} %pad_maximum_fusion.6), channel_id=1, source_target_pairs={{0,8},{1,9},{2,18},{3,19},{4,12},{5,13},{6,22},{7,23},{8,0},{9,1},... | collective-permute-start | bytes 1376264 | tf_op jit(solution)/shard_map/ppermute | solution.py:377
  101.5 15.9 %collective-permute-start.13 = (bf16[256,3584]{1,0:T(8,128)(2,1)S(1)}, bf16[256,3584]{1,0:T(8,128)(2,1)S(1)}, u32[]{:S(2)}, u32[]{:S(2)}) collective-permute-start(bf16[256,3584]{1,0:T(8,128)(2,1)S(1)} %get-tuple-element.61), channel_id=1, source_target_pairs={{0,2},{1,3},{2,0},{3,1},{4,6},{5,7},{6,4},{7,5},{8,10},{9,11},{10,... | collective-permute-start | bytes 5505032 | tf_op jit(solution)/shard_map/ppermute | solution.py:377
  101.7 8.5 %collective-permute-start.18 = (bf16[64,3584]{1,0:T(8,128)(2,1)S(1)}, bf16[64,3584]{1,0:T(8,128)(2,1)S(1)}, u32[]{:S(2)}, u32[]{:S(2)}) collective-permute-start(bf16[64,3584]{1,0:T(8,128)(2,1)S(1)} %pad_maximum_fusion.6), channel_id=1, source_target_pairs={{0,4},{1,5},{2,3},{3,2},{4,0},{5,1},{6,7},{7,6},{8,12},{9,13},{10,... | collective-permute-start | bytes 1376264 | tf_op jit(solution)/shard_map/ppermute | solution.py:377
  106.7 8.5 %collective-permute-start.20 = (bf16[64,3584]{1,0:T(8,128)(2,1)S(1)}, bf16[64,3584]{1,0:T(8,128)(2,1)S(1)}, u32[]{:S(2)}, u32[]{:S(2)}) collective-permute-start(bf16[64,3584]{1,0:T(8,128)(2,1)S(1)} %collective-permute-done.17), channel_id=1, source_target_pairs={{0,4},{1,5},{2,3},{3,2},{4,0},{5,1},{6,7},{7,6},{8,12},{9,13},{10,... | collective-permute-start | bytes 1376264 | tf_op jit(solution)/shard_map/ppermute | solution.py:377
  107.5 17.8 %collective-permute-start.19 = (bf16[64,3584]{1,0:T(8,128)(2,1)S(1)}, bf16[64,3584]{1,0:T(8,128)(2,1)S(1)}, u32[]{:S(2)}, u32[]{:S(2)}) collective-permute-start(bf16[64,3584]{1,0:T(8,128)(2,1)S(1)} %pad_maximum_fusion.6), channel_id=1, source_target_pairs={{0,1},{1,0},{2,10},{3,11},{4,5},{5,4},{6,14},{7,15},{8,9},{9,8},{1... | collective-permute-start | bytes 1376264 | tf_op jit(solution)/shard_map/ppermute | solution.py:377
  110.1 14.2 %collective-permute-start.21 = (bf16[64,3584]{1,0:T(8,128)(2,1)S(1)}, bf16[64,3584]{1,0:T(8,128)(2,1)S(1)}, u32[]{:S(2)}, u32[]{:S(2)}) collective-permute-start(bf16[64,3584]{1,0:T(8,128)(2,1)S(1)} %collective-permute-done.17), channel_id=1, source_target_pairs={{0,1},{1,0},{2,10},{3,11},{4,5},{5,4},{6,14},{7,15},{8,9},{9,8},{1... | collective-permute-start | bytes 1376264 | tf_op jit(solution)/shard_map/ppermute | solution.py:377
  115.1 19.0 %collective-permute-start.24 = (bf16[64,3584]{1,0:T(8,128)(2,1)S(1)}, bf16[64,3584]{1,0:T(8,128)(2,1)S(1)}, u32[]{:S(2)}, u32[]{:S(2)}) collective-permute-start(bf16[64,3584]{1,0:T(8,128)(2,1)S(1)} %collective-permute-done.18), channel_id=1, source_target_pairs={{0,1},{1,0},{2,10},{3,11},{4,5},{5,4},{6,14},{7,15},{8,9},{9,8},{1... | collective-permute-start | bytes 1376264 | tf_op jit(solution)/shard_map/ppermute | solution.py:377
  116.0 18.1 %collective-permute-start.25 = (bf16[64,3584]{1,0:T(8,128)(2,1)S(1)}, bf16[64,3584]{1,0:T(8,128)(2,1)S(1)}, u32[]{:S(2)}, u32[]{:S(2)}) collective-permute-start(bf16[64,3584]{1,0:T(8,128)(2,1)S(1)} %collective-permute-done.20), channel_id=1, source_target_pairs={{0,1},{1,0},{2,10},{3,11},{4,5},{5,4},{6,14},{7,15},{8,9},{9,8},{1... | collective-permute-start | bytes 1376264 | tf_op jit(solution)/shard_map/ppermute | solution.py:377
  117.4 22.2 %collective-permute-start.22 = (bf16[64,3584]{1,0:T(8,128)(2,1)S(1)}, bf16[64,3584]{1,0:T(8,128)(2,1)S(1)}, u32[]{:S(2)}, u32[]{:S(2)}) collective-permute-start(bf16[64,3584]{1,0:T(8,128)(2,1)S(1)} %get-tuple-element.103), channel_id=1, source_target_pairs={{0,1},{1,0},{2,10},{3,11},{4,5},{5,4},{6,14},{7,15},{8,9},{9,8},{1... | collective-permute-start | bytes 1376264 | tf_op jit(solution)/shard_map/ppermute | solution.py:377
  124.3 24.6 %collective-permute-start.29 = (bf16[64,3584]{1,0:T(8,128)(2,1)S(1)}, bf16[64,3584]{1,0:T(8,128)(2,1)S(1)}, u32[]{:S(2)}, u32[]{:S(2)}) collective-permute-start(bf16[64,3584]{1,0:T(8,128)(2,1)S(1)} %get-tuple-element.99), channel_id=1, source_target_pairs={{0,1},{1,0},{2,10},{3,11},{4,5},{5,4},{6,14},{7,15},{8,9},{9,8},{1... | collective-permute-start | bytes 1376264 | tf_op jit(solution)/shard_map/ppermute | solution.py:377
  125.6 26.3 %collective-permute-start.23 = (bf16[256,3584]{1,0:T(8,128)(2,1)S(1)}, bf16[256,3584]{1,0:T(8,128)(2,1)S(1)}, u32[]{:S(2)}, u32[]{:S(2)}) collective-permute-start(bf16[256,3584]{1,0:T(8,128)(2,1)S(1)} %pad_maximum_fusion.near_own), channel_id=1, source_target_pairs={{0,2},{1,3},{2,0},{3,1},{4,6},{5,7},{6,4},{7,5},{8,10},{9,11},{10,... | collective-permute-start | bytes 5505032 | tf_op jit(solution)/shard_map/ppermute | solution.py:377
  134.3 17.6 %collective-permute-start.26 = (bf16[256,3584]{1,0:T(8,128)(2,1)S(1)}, bf16[256,3584]{1,0:T(8,128)(2,1)S(1)}, u32[]{:S(2)}, u32[]{:S(2)}) collective-permute-start(bf16[256,3584]{1,0:T(8,128)(2,1)S(1)} %pad_maximum_fusion.1.near_other), channel_id=1, source_target_pairs={{0,2},{1,3},{2,0},{3,1},{4,6},{5,7},{6,4},{7,5},{8,10},{9,11},{10,... | collective-permute-start | bytes 5505032 | tf_op jit(solution)/shard_map/ppermute | solution.py:377
  140.0 9.9 %collective-permute-start.30 = (bf16[64,3584]{1,0:T(8,128)(2,1)S(1)}, bf16[64,3584]{1,0:T(8,128)(2,1)S(1)}, u32[]{:S(2)}, u32[]{:S(2)}) collective-permute-start(bf16[64,3584]{1,0:T(8,128)(2,1)S(1)} %get-tuple-element.101), channel_id=1, source_target_pairs={{0,4},{1,5},{2,3},{3,2},{4,0},{5,1},{6,7},{7,6},{8,12},{9,13},{10,... | collective-permute-start | bytes 1376264 | tf_op jit(solution)/shard_map/ppermute | solution.py:377
  141.6 22.7 %collective-permute-start.27 = (bf16[64,3584]{1,0:T(8,128)(2,1)S(1)}, bf16[64,3584]{1,0:T(8,128)(2,1)S(1)}, u32[]{:S(2)}, u32[]{:S(2)}) collective-permute-start(bf16[64,3584]{1,0:T(8,128)(2,1)S(1)} %get-tuple-element.102), channel_id=1, source_target_pairs={{0,1},{1,0},{2,10},{3,11},{4,5},{5,4},{6,14},{7,15},{8,9},{9,8},{1... | collective-permute-start | bytes 1376264 | tf_op jit(solution)/shard_map/ppermute | solution.py:377
  148.9 41.9 %collective-permute-start.15 = (bf16[64,3584]{1,0:T(8,128)(2,1)}, bf16[64,3584]{1,0:T(8,128)(2,1)S(1)}, u32[]{:S(2)}, u32[]{:S(2)}) collective-permute-start(bf16[64,3584]{1,0:T(8,128)(2,1)} %get-tuple-element.97), channel_id=1, source_target_pairs={{0,1},{1,0},{2,10},{3,11},{4,5},{5,4},{6,14},{7,15},{8,9},{9,8},{1... | collective-permute-start | bytes 1376264 | tf_op jit(solution)/shard_map/ppermute | solution.py:377
  150.9 41.4 %collective-permute-start.31 = (bf16[64,3584]{1,0:T(8,128)(2,1)}, bf16[64,3584]{1,0:T(8,128)(2,1)}, u32[]{:S(2)}, u32[]{:S(2)}) collective-permute-start(bf16[64,3584]{1,0:T(8,128)(2,1)} %add_convert_fusion), channel_id=1, source_target_pairs={{0,8},{1,9},{2,18},{3,19},{4,12},{5,13},{6,22},{7,23},{8,0},{9,1},... | collective-permute-start | bytes 1376264 | tf_op jit(solution)/shard_map/ppermute | solution.py:377
  165.2 27.0 %collective-permute-start.28 = (bf16[64,3584]{1,0:T(8,128)(2,1)}, bf16[64,3584]{1,0:T(8,128)(2,1)}, u32[]{:S(2)}, u32[]{:S(2)}) collective-permute-start(bf16[64,3584]{1,0:T(8,128)(2,1)} %add_convert_fusion.2), channel_id=1, source_target_pairs={{0,4},{1,5},{2,3},{3,2},{4,0},{5,1},{6,7},{7,6},{8,12},{9,13},{10,... | collective-permute-start | bytes 1376264 | tf_op jit(solution)/shard_map/ppermute | solution.py:377
  166.4 2.1 %copy-start.3 = (bf16[256,3584]{1,0:T(8,128)(2,1)S(1)}, bf16[256,3584]{1,0:T(8,128)(2,1)}, u32[]{:S(2)}) copy-start(bf16[256,3584]{1,0:T(8,128)(2,1)} %copy-done.2) | copy-start | bytes 5505028
  179.4 2.0 copy-start.1
  179.6 3.8 %collective-permute-start.33 = (f32[3584]{0:T(1024)S(1)}, f32[3584]{0:T(1024)S(1)}, u32[]{:S(2)}, u32[]{:S(2)}) collective-permute-start(f32[3584]{0:T(1024)S(1)} %divide_subtract_fusion), channel_id=1, source_target_pairs={{0,1},{1,0},{2,3},{3,2},{4,5},{5,4},{6,7},{7,6},{8,9},{9,8},{10,11... | collective-permute-start | bytes 43016 | tf_op jit(solution)/shard_map/ppermute | solution.py:377
  181.1 2.3 %copy-start.8 = (bf16[3584]{0:T(1024)(128)(2,1)S(1)}, bf16[3584]{0:T(1024)(128)(2,1)}, u32[]{:S(2)}) copy-start(bf16[3584]{0:T(1024)(128)(2,1)} %param.12) | copy-start | bytes 21508
  181.4 21.5 %copy-start.7 = (f32[3584]{0:T(1024)S(1)}, f32[3584]{0:T(1024)}, u32[]{:S(2)}) copy-start(f32[3584]{0:T(1024)} %param.11) | copy-start | bytes 43012
  183.4 3.2 %collective-permute-start.36 = (f32[3584]{0:T(1024)S(1)}, f32[3584]{0:T(1024)S(1)}, u32[]{:S(2)}, u32[]{:S(2)}) collective-permute-start(f32[3584]{0:T(1024)S(1)} %add_add_fusion.2), channel_id=1, source_target_pairs={{0,6},{1,7},{2,4},{3,5},{4,2},{5,3},{6,0},{7,1},{8,14},{9,15},{10,... | collective-permute-start | bytes 43016 | tf_op jit(solution)/shard_map/ppermute | solution.py:377
  183.5 3.9 %collective-permute-start.35 = (f32[3584]{0:T(1024)S(1)}, f32[3584]{0:T(1024)S(1)}, u32[]{:S(2)}, u32[]{:S(2)}) collective-permute-start(f32[3584]{0:T(1024)S(1)} %add_add_fusion.2), channel_id=1, source_target_pairs={{0,4},{1,5},{2,6},{3,7},{4,0},{5,1},{6,2},{7,3},{8,12},{9,13},{10,... | collective-permute-start | bytes 43016 | tf_op jit(solution)/shard_map/ppermute | solution.py:377
  186.7 1.2 collective-permute-start.34
  187.8 7.0 %collective-permute-start.39 = (f32[3584]{0:T(1024)S(1)}, f32[3584]{0:T(1024)S(1)}, u32[]{:S(2)}, u32[]{:S(2)}) collective-permute-start(f32[3584]{0:T(1024)S(1)} %add_add_fusion.1), channel_id=1, source_target_pairs={{0,24},{1,25},{2,26},{3,27},{4,28},{5,29},{6,30},{7,31},{8,16},{9,... | collective-permute-start | bytes 43016 | tf_op jit(solution)/shard_map/ppermute | solution.py:377
  189.5 5.3 %collective-permute-start.38 = (f32[3584]{0:T(1024)S(1)}, f32[3584]{0:T(1024)S(1)}, u32[]{:S(2)}, u32[]{:S(2)}) collective-permute-start(f32[3584]{0:T(1024)S(1)} %add_add_fusion.1), channel_id=1, source_target_pairs={{0,16},{1,17},{2,18},{3,19},{4,20},{5,21},{6,22},{7,23},{8,24},{9,... | collective-permute-start | bytes 43016 | tf_op jit(solution)/shard_map/ppermute | solution.py:377
  190.8 4.1 %collective-permute-start.37 = (f32[3584]{0:T(1024)S(1)}, f32[3584]{0:T(1024)S(1)}, u32[]{:S(2)}, u32[]{:S(2)}) collective-permute-start(f32[3584]{0:T(1024)S(1)} %add_add_fusion.1), channel_id=1, source_target_pairs={{0,8},{1,9},{2,10},{3,11},{4,12},{5,13},{6,14},{7,15},{8,0},{9,1},... | collective-permute-start | bytes 43016 | tf_op jit(solution)/shard_map/ppermute | solution.py:377
  193.4 9.4 %collective-permute-start.32 = (bf16[32,3584]{1,0:T(8,128)(2,1)S(1)}, bf16[32,3584]{1,0:T(8,128)(2,1)S(1)}, u32[]{:S(2)}, u32[]{:S(2)}) collective-permute-start(bf16[32,3584]{1,0:T(8,128)(2,1)S(1)} %add_convert_fusion.12), channel_id=1, source_target_pairs={{0,16},{1,17},{2,6},{3,7},{4,20},{5,21},{6,2},{7,3},{8,24},{9,25},... | collective-permute-start | bytes 688136 | tf_op jit(solution)/shard_map/ppermute | solution.py:377
  (1 other events, 1.2 us)
